TPU v7x, 8 devices: a whole 2x2x1 slice. The times are simulated.
8 devices in a mesh: data: 4 (over z, y, x), pipe: 2 (over core).
Axes of the slice: x: 2, y: 2, z: 1, core: 2. Of those that a mesh axis runs over, the one named last changes fastest.
Arguments:
- acts_in: bfloat16 [128, 64, 1280], P(('data', 'pipe'))
- cot_out: bfloat16 [128, 64, 1280], P(('data', 'pipe'))
- seq_lens: int32 [128], P(('data', 'pipe'))
- w_qkv: bfloat16 [2, 1280, 3840], P('pipe')
- w_out: bfloat16 [2, 20, 64, 1280], P('pipe')
- w_up: bfloat16 [2, 1280, 5120], P('pipe')
- w_down: bfloat16 [2, 5120, 1280], P('pipe')
- gain_attn: bfloat16 [2, 1280], P('pipe')
- gain_mlp: bfloat16 [2, 1280], P('pipe')
Outputs:
- output 1: bfloat16 [128, 64, 1280], P(('data', 'pipe'))
- output 2: float32 [2, 1280, 3840], P('pipe')
- output 3: float32 [2, 20, 64, 1280], P('pipe')
- output 4: float32 [2, 1280, 5120], P('pipe')
- output 5: float32 [2, 5120, 1280], P('pipe')
- output 6: float32 [2, 1280], P('pipe')
- output 7: float32 [2, 1280], P('pipe')
All inputs are finite; a program needn't handle non-finite values.
Results may differ from a plain program's by a relative error of at most 0.02.
Values are sent between devices in bfloat16 or wider.
A program may use at most 1 GiB of HBM per device.

v0:
```python
import functools
import jax
import jax.numpy as jnp
from jax import lax
from jax.sharding import PartitionSpec as P, NamedSharding

NORM_EPS = 1e-5


def norm_f32(hid_f32, gain_f32):
    inv_rms = lax.rsqrt(jnp.mean(hid_f32 * hid_f32, axis=-1, keepdims=True) + NORM_EPS)
    return hid_f32 * inv_rms * gain_f32


def attention_core(q_heads, k_heads, v_heads, visible):
    scale = q_heads.shape[-1] ** -0.5
    scores = jnp.einsum('mqhe,mkhe->mhqk', q_heads, k_heads, preferred_element_type=jnp.float32) * scale
    scores = jnp.where(visible[:, None], scores, -1e30)
    attn_probs = jax.nn.softmax(scores, axis=-1).astype(jnp.bfloat16)
    return jnp.einsum('mhqk,mkhe->mqhe', attn_probs, v_heads, preferred_element_type=jnp.float32).astype(jnp.bfloat16)


def layer_forward(hidden, layer_w, visible):
    w_qkv, w_out, w_up, w_down, gain_attn, gain_mlp = layer_w
    n_micro, seq_size = hidden.shape[0], hidden.shape[1]
    heads, head_dim = w_out.shape[0], w_out.shape[1]
    hid_f32 = hidden.astype(jnp.float32)
    normed_a = norm_f32(hid_f32, gain_attn.astype(jnp.float32)).astype(jnp.bfloat16)
    qkv_all = jnp.einsum('msd,de->mse', normed_a, w_qkv, preferred_element_type=jnp.float32)
    qkv_all = qkv_all.astype(jnp.bfloat16).reshape(n_micro, seq_size, 3, heads, head_dim)
    context = attention_core(qkv_all[:, :, 0], qkv_all[:, :, 1], qkv_all[:, :, 2], visible)
    attn_out = jnp.einsum('mshe,hed->msd', context, w_out, preferred_element_type=jnp.float32)
    mid_hidden = (hid_f32 + attn_out).astype(jnp.bfloat16)
    mid_up = mid_hidden.astype(jnp.float32)
    normed_m = norm_f32(mid_up, gain_mlp.astype(jnp.float32)).astype(jnp.bfloat16)
    pre_act = jnp.einsum('msd,df->msf', normed_m, w_up, preferred_element_type=jnp.float32)
    gelu_out = jax.nn.gelu(pre_act, approximate=False).astype(jnp.bfloat16)
    mlp_out = jnp.einsum('msf,fd->msd', gelu_out, w_down, preferred_element_type=jnp.float32)
    out_hidden = (mid_up + mlp_out).astype(jnp.bfloat16)
    saved = (hidden, normed_a, qkv_all, context, mid_hidden, normed_m, pre_act, gelu_out)
    return out_hidden, saved


def layer_backward(d_hidden, saved, layer_w, visible):
    w_qkv, w_out, w_up, w_down, gain_attn, gain_mlp = layer_w
    hidden, normed_a, qkv_all, context, mid_hidden, normed_m, pre_act, gelu_out = saved
    n_micro, seq_size = hidden.shape[0], hidden.shape[1]
    d_top = d_hidden.astype(jnp.bfloat16)
    grad_down = jnp.einsum('msf,msd->fd', gelu_out, d_top, preferred_element_type=jnp.float32)
    d_gelu = jnp.einsum('msd,fd->msf', d_top, w_down, preferred_element_type=jnp.float32)
    gelu_pull = jax.vjp(functools.partial(jax.nn.gelu, approximate=False), pre_act)[1]
    d_pre = gelu_pull(d_gelu)[0].astype(jnp.bfloat16)
    grad_up = jnp.einsum('msd,msf->df', normed_m, d_pre, preferred_element_type=jnp.float32)
    d_normed_m = jnp.einsum('msf,df->msd', d_pre, w_up, preferred_element_type=jnp.float32)
    norm_pull_m = jax.vjp(norm_f32, mid_hidden.astype(jnp.float32), gain_mlp.astype(jnp.float32))[1]
    d_mid_norm, grad_gain_mlp = norm_pull_m(d_normed_m)
    d_mid = d_hidden + d_mid_norm
    d_mid_bf = d_mid.astype(jnp.bfloat16)
    grad_out = jnp.einsum('mshe,msd->hed', context, d_mid_bf, preferred_element_type=jnp.float32)
    d_context = jnp.einsum('msd,hed->mshe', d_mid_bf, w_out, preferred_element_type=jnp.float32).astype(jnp.bfloat16)
    attn_pull = jax.vjp(lambda q_in, k_in, v_in: attention_core(q_in, k_in, v_in, visible), qkv_all[:, :, 0], qkv_all[:, :, 1], qkv_all[:, :, 2])[1]
    d_query, d_key, d_value = attn_pull(d_context)
    d_qkv = jnp.stack([d_query, d_key, d_value], axis=2).reshape(n_micro, seq_size, -1)
    grad_qkv = jnp.einsum('msd,mse->de', normed_a, d_qkv, preferred_element_type=jnp.float32)
    d_normed_a = jnp.einsum('mse,de->msd', d_qkv, w_qkv, preferred_element_type=jnp.float32)
    norm_pull_a = jax.vjp(norm_f32, hidden.astype(jnp.float32), gain_attn.astype(jnp.float32))[1]
    d_in_norm, grad_gain_attn = norm_pull_a(d_normed_a)
    return d_mid + d_in_norm, (grad_qkv, grad_out, grad_up, grad_down, grad_gain_attn, grad_gain_mlp)


def stage_forward(hidden, stage_w, visible):
    for layer_idx in range(stage_w[0].shape[0]):
        hidden = layer_forward(hidden, tuple(w_part[layer_idx] for w_part in stage_w), visible)[0]
    return hidden


def stage_backward(stage_in, d_hidden, stage_w, visible):
    num_local = stage_w[0].shape[0]
    saved_all = []
    hidden = stage_in
    for layer_idx in range(num_local):
        hidden, saved_acts = layer_forward(hidden, tuple(w_part[layer_idx] for w_part in stage_w), visible)
        saved_all.append(saved_acts)
    grads_rev = []
    for layer_idx in reversed(range(num_local)):
        d_hidden, layer_grads = layer_backward(d_hidden, saved_all[layer_idx], tuple(w_part[layer_idx] for w_part in stage_w), visible)
        grads_rev.append(layer_grads)
    grads_by_layer = grads_rev[::-1]
    stage_grads = tuple(jnp.stack([layer_grads[part_idx] for layer_grads in grads_by_layer]) for part_idx in range(6))
    return d_hidden, stage_grads


def solution(mesh):
    row_spec = P(('data', 'pipe'))
    stage_spec = P('pipe')
    pipe_size = mesh.shape['pipe']
    num_slots = 2 * pipe_size - 1
    fwd_perm = [(src_dev, (src_dev - 1) % pipe_size) for src_dev in range(pipe_size)]
    bwd_perm = [(src_dev, (src_dev + 1) % pipe_size) for src_dev in range(pipe_size)]
    home_shift = 2 % pipe_size
    home_perm = [(src_dev, (src_dev + home_shift) % pipe_size) for src_dev in range(pipe_size)]

    def device_pass(acts_in, cot_out, seq_lens, w_qkv, w_out, w_up, w_down, gain_attn, gain_mlp):
        own_w = (w_qkv, w_out, w_up, w_down, gain_attn, gain_mlp)
        pipe_pos = lax.axis_index('pipe')
        fwd_offset = (pipe_size - pipe_pos) % pipe_size
        bwd_offset = (pipe_pos + 1) % pipe_size
        positions = jnp.arange(acts_in.shape[1])
        causal = positions[None, None, :] <= positions[None, :, None]
        visible = causal & (positions[None, None, :] < seq_lens[:, None, None])
        valid = (positions[None, :] < seq_lens[:, None])[:, :, None]

        def fwd_slot(slot, hidden, stage_inputs, held_w):
            slot_rel = slot - fwd_offset
            active = (slot_rel >= 0) & (slot_rel < pipe_size)
            stage_idx = jnp.clip(slot_rel, 0, pipe_size - 1)

            def run_stage(operands):
                hid_state, inputs_buf = operands
                inputs_buf = lax.dynamic_update_index_in_dim(inputs_buf, hid_state, stage_idx, 0)
                return stage_forward(hid_state, held_w, visible), inputs_buf

            return lax.cond(active, run_stage, lambda operands: operands, (hidden, stage_inputs))

        def fwd_body(slot, loop_carry):
            hidden, stage_inputs, held_w = loop_carry
            held_w = tuple(lax.ppermute(w_part, 'pipe', fwd_perm) for w_part in held_w)
            hidden, stage_inputs = fwd_slot(slot, hidden, stage_inputs, held_w)
            return hidden, stage_inputs, held_w

        stage_inputs = jnp.zeros((pipe_size,) + acts_in.shape, acts_in.dtype)
        hidden, stage_inputs = fwd_slot(0, acts_in, stage_inputs, own_w)
        hidden, stage_inputs, _ = lax.fori_loop(1, num_slots, fwd_body, (hidden, stage_inputs, own_w))
        acts_out = jnp.where(valid, hidden, jnp.zeros_like(hidden))

        def bwd_slot(slot, d_hidden, held_w, held_acc):
            slot_rel = slot - bwd_offset
            active = (slot_rel >= 0) & (slot_rel < pipe_size)
            stage_idx = pipe_size - 1 - jnp.clip(slot_rel, 0, pipe_size - 1)

            def run_stage(operands):
                d_state, acc_in = operands
                stage_in = lax.dynamic_index_in_dim(stage_inputs, stage_idx, 0, keepdims=False)
                d_new, stage_grads = stage_backward(stage_in, d_state, held_w, visible)
                return d_new, tuple(acc_part + grad_part for acc_part, grad_part in zip(acc_in, stage_grads))

            return lax.cond(active, run_stage, lambda operands: operands, (d_hidden, held_acc))

        def bwd_body(slot, loop_carry):
            d_hidden, held_w, held_acc = loop_carry
            held_w = tuple(lax.ppermute(w_part, 'pipe', bwd_perm) for w_part in held_w)
            held_acc = tuple(lax.ppermute(acc_part, 'pipe', bwd_perm) for acc_part in held_acc)
            d_hidden, held_acc = bwd_slot(slot, d_hidden, held_w, held_acc)
            return d_hidden, held_w, held_acc

        d_hidden = jnp.where(valid, cot_out.astype(jnp.float32), 0.0)
        zero_acc = tuple(jnp.zeros(w_part.shape, jnp.float32) for w_part in own_w)
        d_hidden, held_acc = bwd_slot(0, d_hidden, own_w, zero_acc)
        _, _, held_acc = lax.fori_loop(1, num_slots, bwd_body, (d_hidden, own_w, held_acc))
        if home_shift:
            held_acc = tuple(lax.ppermute(acc_part, 'pipe', home_perm) for acc_part in held_acc)
        grads = tuple(lax.psum(acc_part, 'data') for acc_part in held_acc)
        return (acts_out,) + grads

    return jax.shard_map(device_pass, mesh=mesh, in_specs=(row_spec, row_spec, row_spec) + (stage_spec,) * 6, out_specs=(row_spec,) + (stage_spec,) * 6, check_vma=False)
```

profile of v0, /device:TPU:0, one launch (start us, length us, event | category | flops | bytes accessed | tf_op | source)
XLA Modules:
  0.0 4063.3 jit_solution(12675717738423553955)
XLA Ops:
  70.8 186.1 %conditional.4 = (bf16[16,64,1280]{2,1,0:T(8,128)(2,1)S(1)}, bf16[2,16,64,1280]{3,2,1,0:T(8,128)(2,1)}) conditional(s32[]{:T(128)} %convert_element_type.343, bf16[16,64,1280]{2,1,0:T(8,128)(2,1)S(1)} %copy-done.5, (bf16[16,64,1280]{2,1,0:T(8,128)(2,1)S(1)}, bf16[1,1280]{1,0:T(2,128)(2,1)S(1)}, bf16[1,1280,3840]{2,1,0:T(8,128)(2,1)}, ...), branch_computations={%region_0.1_spmd, %region_1.6_spmd} | conditional | flops 41077313536 | bytes 230974624 | solution.py:123
  191.7 65.0 %fusion.34 = bf16[16,64,1280]{2,1,0:T(8,128)(2,1)S(1)} fusion(bf16[16,64,1280]{2,1,0:T(8,128)(2,1)S(1)} %copy-done.79, bf16[1,5120,1280]{2,1,0:T(8,128)(2,1)} %get-tuple-element.577, f32[16,64,5120]{2,1,0:T(8,128)} %get-tuple-element.873, u16[64,5120]{1,0:T(8,128)(2,1)S(1)} %get-tuple-element.785, u16[64,5120]{1,0:T(8,128)(2,1)S(1)} %get-tuple-element.784), kind=kOutput, calls=%fused_computation.52 | convolution fusion | flops 13792706560 | bytes 40632320 | tf_op jit(solution)/shard_map/cond/branch_1_fun/msf,fd->msd/dot_general | solution.py:38
  257.0 387.4 %while.66 = (s32[]{:T(128)}, bf16[16,64,1280]{2,1,0:T(8,128)(2,1)S(1)}, bf16[2,16,64,1280]{3,2,1,0:T(8,128)(2,1)}, bf16[1,1280,3840]{2,1,0:T(8,128)(2,1)}, bf16[...) while((s32[]{:T(128)}, ...), condition=%wide.region_13.14_spmd.clone, body=%wide.region_6.13_spmd.clone.sunk | while | flops 41077379072 | bytes 443433696 | solution.py:133
  267.2 56.3 %collective-permute-done = bf16[1,1280]{1,0:T(2,128)(2,1)S(1)} collective-permute-done((bf16[1,1280]{1,0:T(2,128)(2,1)S(1)}, bf16[1,1280]{1,0:T(2,128)(2,1)S(1)}, u32[]{:S(2)}, u32[]{:S(2)}) %collective-permute-start) | collective-permute-done | bytes 2592 | tf_op jit(solution)/shard_map/while/body/eval_jaxpr/ppermute | solution.py:127
  337.3 182.3 %conditional.10 = ((bf16[16,64,1280]{2,1,0:T(8,128)(2,1)S(1)}, bf16[2,16,64,1280]{3,2,1,0:T(8,128)(2,1)})) conditional(s32[]{:T(128)} %convert_element_type.707, (bf16[16,64,1280]{2,1,0:T(8,128)(2,1)S(1)}, bf16[2,16,64,1280]{3,2,1,0:T(8,128)(2,1)}) %tuple.141, (bf16[16,64,1280]{2,1,0:T(8,128)(2,1)S(1)}, bf16[1,1280]{1,0:T(2,128)(2,1)S(1)}, ...), branch_computations={%region_7.7_spmd, %region_8.12_spmd} | conditional | flops 41077379072 | bytes 207452320 | solution.py:123
  454.2 65.1 %fusion.129 = bf16[16,64,1280]{2,1,0:T(8,128)(2,1)S(1)} fusion(bf16[16,64,1280]{2,1,0:T(8,128)(2,1)S(1)} %copy-done.80, bf16[1,5120,1280]{2,1,0:T(8,128)(2,1)} %get-tuple-element.586, f32[16,64,5120]{2,1,0:T(8,128)} %get-tuple-element.883, u16[64,5120]{1,0:T(8,128)(2,1)S(1)} %get-tuple-element.787, u16[64,5120]{1,0:T(8,128)(2,1)S(1)} %get-tuple-element.786), kind=kOutput, calls=%fused_computation.160 | convolution fusion | flops 13792706560 | bytes 40632320 | tf_op jit(solution)/shard_map/while/body/eval_jaxpr/cond/branch_1_fun/msf,fd->msd/dot_general | solution.py:38
  543.0 56.0 %collective-permute-done = bf16[1,1280]{1,0:T(2,128)(2,1)S(1)} collective-permute-done((bf16[1,1280]{1,0:T(2,128)(2,1)S(1)}, bf16[1,1280]{1,0:T(2,128)(2,1)S(1)}, u32[]{:S(2)}, u32[]{:S(2)}) %collective-permute-start) | collective-permute-done | bytes 2592 | tf_op jit(solution)/shard_map/while/body/eval_jaxpr/ppermute | solution.py:127
  645.9 36.5 conditional.5
  683.0 2027.9 %while.67 = (s32[]{:T(128)}, f32[16,64,1280]{2,1,0:T(8,128)}, bf16[1,1280,3840]{2,1,0:T(8,128)(2,1)}, bf16[1,20,64,1280]{3,2,1,0:T(8,128)(2,1)}, bf16[1,1280,512...) while((s32[]{:T(128)}, f32[16,64,1280]{2,1,0:T(8,128)}, ...), condition=%wide.region_37.38_spmd.clone, body=%wide.region_25.37_spmd.clone.sunk | while | flops 109036953600 | bytes 1550642816 | solution.py:159
  688.5 586.5 %collective-permute-start.8 = (f32[1,1280,5120]{2,1,0:T(8,128)}, f32[1,1280,5120]{2,1,0:T(8,128)}, u32[]{:S(2)}, u32[]{:S(2)}) collective-permute-start(f32[1,1280,5120]{2,1,0:T(8,128)} %get-tuple-element.1226), channel_id=1, source_target_pairs={{0,1},{1,0},{2,3},{3,2},{4,5},{5,4},{6,7},{7,6}} | collective-permute-start | bytes 78643208 | tf_op jit(solution)/shard_map/while/body/eval_jaxpr/ppermute | solution.py:152
  1276.0 93.5 %collective-permute-done.12 = bf16[1,1280]{1,0:T(2,128)(2,1)S(1)} collective-permute-done((bf16[1,1280]{1,0:T(2,128)(2,1)}, bf16[1,1280]{1,0:T(2,128)(2,1)S(1)}, u32[]{:S(2)}, u32[]{:S(2)}) %collective-permute-start.12) | collective-permute-done | bytes 2592 | tf_op jit(solution)/shard_map/while/body/eval_jaxpr/ppermute | solution.py:151
  1392.1 46.5 %collective-permute-done.17 = bf16[1,5120,1280]{2,1,0:T(8,128)(2,1)} collective-permute-done((bf16[1,5120,1280]{2,1,0:T(8,128)(2,1)}, bf16[1,5120,1280]{2,1,0:T(8,128)(2,1)}, u32[]{:S(2)}, u32[]{:S(2)}) %collective-permute-start.17) | collective-permute-done | bytes 13107232 | tf_op jit(solution)/shard_map/while/body/eval_jaxpr/ppermute | solution.py:151
  1472.1 461.4 %conditional.11 = ((f32[16,64,1280]{2,1,0:T(8,128)}, f32[1,1280,3840]{2,1,0:T(8,128)}, f32[1,20,64,1280]{3,2,1,0:T(8,128)}, f32[1,1280,5120]{2,1,0:T(8,128)}, f3...) conditional(s32[]{:T(128)} %convert_element_type.708, (f32[16,64,1280]{2,1,0:T(8,128)}, ...), branch_computations={%region_26.26_spmd, %region_27.0_spmd} | conditional | flops 109036953600 | bytes 842670912 | solution.py:147
  1607.9 47.1 %fusion.309 = f32[16,64,5120]{2,1,0:T(8,128)} fusion(f32[16,64,5120]{2,1,0:T(8,128)} %get-tuple-element.907, u16[64,5120]{1,0:T(8,128)(2,1)S(1)} %get-tuple-element.795, u16[64,5120]{1,0:T(8,128)(2,1)S(1)} %get-tuple-element.794), kind=kLoop, calls=%fused_computation.355 | loop fusion | flops 351272960 | bytes 43253760 | tf_op jit(solution)/shard_map/while/body/eval_jaxpr/cond/branch_1_fun/jvp()/erfc | solution.py:51
  1655.1 36.7 bitcast_add_fusion
  1691.8 30.1 add_convert_fusion.1
  1904.9 27.7 bitcast_add_fusion.1
  1993.3 93.8 %collective-permute-done.12 = bf16[1,1280]{1,0:T(2,128)(2,1)S(1)} collective-permute-done((bf16[1,1280]{1,0:T(2,128)(2,1)}, bf16[1,1280]{1,0:T(2,128)(2,1)S(1)}, u32[]{:S(2)}, u32[]{:S(2)}) %collective-permute-start.12) | collective-permute-done | bytes 2592 | tf_op jit(solution)/shard_map/while/body/eval_jaxpr/ppermute | solution.py:151
  2109.4 46.7 %collective-permute-done.17 = bf16[1,5120,1280]{2,1,0:T(8,128)(2,1)} collective-permute-done((bf16[1,5120,1280]{2,1,0:T(8,128)(2,1)}, bf16[1,5120,1280]{2,1,0:T(8,128)(2,1)}, u32[]{:S(2)}, u32[]{:S(2)}) %collective-permute-start.17) | collective-permute-done | bytes 13107232 | tf_op jit(solution)/shard_map/while/body/eval_jaxpr/ppermute | solution.py:151
  2189.5 461.4 %conditional.11 = ((f32[16,64,1280]{2,1,0:T(8,128)}, f32[1,1280,3840]{2,1,0:T(8,128)}, f32[1,20,64,1280]{3,2,1,0:T(8,128)}, f32[1,1280,5120]{2,1,0:T(8,128)}, f3...) conditional(s32[]{:T(128)} %convert_element_type.708, (f32[16,64,1280]{2,1,0:T(8,128)}, ...), branch_computations={%region_26.26_spmd, %region_27.0_spmd} | conditional | flops 109036953600 | bytes 842670912 | solution.py:147
  2325.2 47.1 %fusion.309 = f32[16,64,5120]{2,1,0:T(8,128)} fusion(f32[16,64,5120]{2,1,0:T(8,128)} %get-tuple-element.907, u16[64,5120]{1,0:T(8,128)(2,1)S(1)} %get-tuple-element.795, u16[64,5120]{1,0:T(8,128)(2,1)S(1)} %get-tuple-element.794), kind=kLoop, calls=%fused_computation.355 | loop fusion | flops 351272960 | bytes 43253760 | tf_op jit(solution)/shard_map/while/body/eval_jaxpr/cond/branch_1_fun/jvp()/erfc | solution.py:51
  2372.3 36.7 bitcast_add_fusion
  2409.0 30.1 add_convert_fusion.1
  2732.4 1271.8 %all-reduce.4.cloned.1.call-done = (f32[1,1280,3840]{2,1,0:T(8,128)}, f32[1,20,64,1280]{3,2,1,0:T(8,128)}, f32[1,1280,5120]{2,1,0:T(8,128)}, f32[1,5120,1280]{2,1,0:T(8,128)}) async-done(((f32[1,1280,3840]{2,1,0:T(8,128)}, f32[1,20,64,1280]{3,2,1,0:T(8,128)}, f32[1,1280,5120]{2,1,0:T(8,128)}, f32[1,5120,1280]{2,1,0:T(8,128)}), (f32[1,1280,3840]{2,1,0:T(8,128)}, f32[1,20,64,1280]{3,2,1,0:T(8,128)}, ...) | async-done | bytes 78643216 | tf_op jit(solution)/shard_map/psum | solution.py:162
  (486 shorter events, 1382.6 us)
Async XLA Ops:
  7.2 3997.0 %all-reduce.4.cloned.1.call-start = ((), (), s32[]{:S(2)}) async-start(), calls=%async_computation | async-start | bytes 157286400 | tf_op jit(solution)/shard_map/psum | solution.py:162
  266.1 71.2 %collective-permute-start.4 = (bf16[1,1280,5120]{2,1,0:T(8,128)(2,1)}, bf16[1,1280,5120]{2,1,0:T(8,128)(2,1)}, u32[]{:S(2)}, u32[]{:S(2)}) collective-permute-start(bf16[1,1280,5120]{2,1,0:T(8,128)(2,1)} %get-tuple-element.1156), channel_id=1, source_target_pairs={{0,1},{1,0},{2,3},{3,2},{4,5},{5,4},{6,7},{7,6}} | collective-permute-start | bytes 39321608 | tf_op jit(solution)/shard_map/while/body/eval_jaxpr/ppermute | solution.py:127
  266.2 71.2 %collective-permute-start.5 = (bf16[1,5120,1280]{2,1,0:T(8,128)(2,1)}, bf16[1,5120,1280]{2,1,0:T(8,128)(2,1)}, u32[]{:S(2)}, u32[]{:S(2)}) collective-permute-start(bf16[1,5120,1280]{2,1,0:T(8,128)(2,1)} %get-tuple-element.1157), channel_id=1, source_target_pairs={{0,1},{1,0},{2,3},{3,2},{4,5},{5,4},{6,7},{7,6}} | collective-permute-start | bytes 39321608 | tf_op jit(solution)/shard_map/while/body/eval_jaxpr/ppermute | solution.py:127
  266.7 62.6 %collective-permute-start.1 = (bf16[1,1280,3840]{2,1,0:T(8,128)(2,1)}, bf16[1,1280,3840]{2,1,0:T(8,128)(2,1)}, u32[]{:S(2)}, u32[]{:S(2)}) collective-permute-start(bf16[1,1280,3840]{2,1,0:T(8,128)(2,1)} %get-tuple-element.1154), channel_id=1, source_target_pairs={{0,1},{1,0},{2,3},{3,2},{4,5},{5,4},{6,7},{7,6}} | collective-permute-start | bytes 29491208 | tf_op jit(solution)/shard_map/while/body/eval_jaxpr/ppermute | solution.py:127
  266.7 58.6 %collective-permute-start.2 = (bf16[1,20,64,1280]{3,2,1,0:T(8,128)(2,1)}, bf16[1,20,64,1280]{3,2,1,0:T(8,128)(2,1)}, u32[]{:S(2)}, u32[]{:S(2)}) collective-permute-start(bf16[1,20,64,1280]{3,2,1,0:T(8,128)(2,1)} %get-tuple-element.1155), channel_id=1, source_target_pairs={{0,1},{1,0},{2,3},{3,2},{4,5},{5,4},{6,7},{7,6}} | collective-permute-start | bytes 9830408 | tf_op jit(solution)/shard_map/while/body/eval_jaxpr/ppermute | solution.py:127
  541.4 71.4 %collective-permute-start.4 = (bf16[1,1280,5120]{2,1,0:T(8,128)(2,1)}, bf16[1,1280,5120]{2,1,0:T(8,128)(2,1)}, u32[]{:S(2)}, u32[]{:S(2)}) collective-permute-start(bf16[1,1280,5120]{2,1,0:T(8,128)(2,1)} %get-tuple-element.1156), channel_id=1, source_target_pairs={{0,1},{1,0},{2,3},{3,2},{4,5},{5,4},{6,7},{7,6}} | collective-permute-start | bytes 39321608 | tf_op jit(solution)/shard_map/while/body/eval_jaxpr/ppermute | solution.py:127
  542.0 70.8 %collective-permute-start.5 = (bf16[1,5120,1280]{2,1,0:T(8,128)(2,1)}, bf16[1,5120,1280]{2,1,0:T(8,128)(2,1)}, u32[]{:S(2)}, u32[]{:S(2)}) collective-permute-start(bf16[1,5120,1280]{2,1,0:T(8,128)(2,1)} %get-tuple-element.1157), channel_id=1, source_target_pairs={{0,1},{1,0},{2,3},{3,2},{4,5},{5,4},{6,7},{7,6}} | collective-permute-start | bytes 39321608 | tf_op jit(solution)/shard_map/while/body/eval_jaxpr/ppermute | solution.py:127
  542.0 62.7 %collective-permute-start.1 = (bf16[1,1280,3840]{2,1,0:T(8,128)(2,1)}, bf16[1,1280,3840]{2,1,0:T(8,128)(2,1)}, u32[]{:S(2)}, u32[]{:S(2)}) collective-permute-start(bf16[1,1280,3840]{2,1,0:T(8,128)(2,1)} %get-tuple-element.1154), channel_id=1, source_target_pairs={{0,1},{1,0},{2,3},{3,2},{4,5},{5,4},{6,7},{7,6}} | collective-permute-start | bytes 29491208 | tf_op jit(solution)/shard_map/while/body/eval_jaxpr/ppermute | solution.py:127
  688.5 783.1 %collective-permute-start.8 = (f32[1,1280,5120]{2,1,0:T(8,128)}, f32[1,1280,5120]{2,1,0:T(8,128)}, u32[]{:S(2)}, u32[]{:S(2)}) collective-permute-start(f32[1,1280,5120]{2,1,0:T(8,128)} %get-tuple-element.1226), channel_id=1, source_target_pairs={{0,1},{1,0},{2,3},{3,2},{4,5},{5,4},{6,7},{7,6}} | collective-permute-start | bytes 78643208 | tf_op jit(solution)/shard_map/while/body/eval_jaxpr/ppermute | solution.py:152
  1275.0 196.6 %collective-permute-start.9 = (f32[1,5120,1280]{2,1,0:T(8,128)}, f32[1,5120,1280]{2,1,0:T(8,128)}, u32[]{:S(2)}, u32[]{:S(2)}) collective-permute-start(f32[1,5120,1280]{2,1,0:T(8,128)} %get-tuple-element.1227), channel_id=1, source_target_pairs={{0,1},{1,0},{2,3},{3,2},{4,5},{5,4},{6,7},{7,6}} | collective-permute-start | bytes 78643208 | tf_op jit(solution)/shard_map/while/body/eval_jaxpr/ppermute | solution.py:152
  1275.0 97.4 %collective-permute-start.13 = (bf16[1,1280,3840]{2,1,0:T(8,128)(2,1)}, bf16[1,1280,3840]{2,1,0:T(8,128)(2,1)}, u32[]{:S(2)}, u32[]{:S(2)}) collective-permute-start(bf16[1,1280,3840]{2,1,0:T(8,128)(2,1)} %get-tuple-element.1218), channel_id=1, source_target_pairs={{0,1},{1,0},{2,3},{3,2},{4,5},{5,4},{6,7},{7,6}} | collective-permute-start | bytes 29491208 | tf_op jit(solution)/shard_map/while/body/eval_jaxpr/ppermute | solution.py:151
  1275.5 96.7 %collective-permute-start.14 = (bf16[1,20,64,1280]{3,2,1,0:T(8,128)(2,1)}, bf16[1,20,64,1280]{3,2,1,0:T(8,128)(2,1)S(1)}, u32[]{:S(2)}, u32[]{:S(2)}) collective-permute-start(bf16[1,20,64,1280]{3,2,1,0:T(8,128)(2,1)} %get-tuple-element.1219), channel_id=1, source_target_pairs={{0,1},{1,0},{2,3},{3,2},{4,5},{5,4},{6,7},{7,6}} | collective-permute-start | bytes 9830408 | tf_op jit(solution)/shard_map/while/body/eval_jaxpr/ppermute | solution.py:151
  1275.5 94.0 %collective-permute-start.12 = (bf16[1,1280]{1,0:T(2,128)(2,1)}, bf16[1,1280]{1,0:T(2,128)(2,1)S(1)}, u32[]{:S(2)}, u32[]{:S(2)}) collective-permute-start(bf16[1,1280]{1,0:T(2,128)(2,1)} %get-tuple-element.1222), channel_id=1, source_target_pairs={{0,1},{1,0},{2,3},{3,2},{4,5},{5,4},{6,7},{7,6}} | collective-permute-start | bytes 7688 | tf_op jit(solution)/shard_map/while/body/eval_jaxpr/ppermute | solution.py:151
  1372.2 99.3 %collective-permute-start.6 = (f32[1,1280,3840]{2,1,0:T(8,128)}, f32[1,1280,3840]{2,1,0:T(8,128)}, u32[]{:S(2)}, u32[]{:S(2)}) collective-permute-start(f32[1,1280,3840]{2,1,0:T(8,128)} %get-tuple-element.1224), channel_id=1, source_target_pairs={{0,1},{1,0},{2,3},{3,2},{4,5},{5,4},{6,7},{7,6}} | collective-permute-start | bytes 58982408 | tf_op jit(solution)/shard_map/while/body/eval_jaxpr/ppermute | solution.py:152
  1372.4 66.2 %collective-permute-start.17 = (bf16[1,5120,1280]{2,1,0:T(8,128)(2,1)}, bf16[1,5120,1280]{2,1,0:T(8,128)(2,1)}, u32[]{:S(2)}, u32[]{:S(2)}) collective-permute-start(bf16[1,5120,1280]{2,1,0:T(8,128)(2,1)} %get-tuple-element.1221), channel_id=1, source_target_pairs={{0,1},{1,0},{2,3},{3,2},{4,5},{5,4},{6,7},{7,6}} | collective-permute-start | bytes 39321608 | tf_op jit(solution)/shard_map/while/body/eval_jaxpr/ppermute | solution.py:151
  1391.7 79.8 %collective-permute-start.7 = (f32[1,20,64,1280]{3,2,1,0:T(8,128)}, f32[1,20,64,1280]{3,2,1,0:T(8,128)}, u32[]{:S(2)}, u32[]{:S(2)}) collective-permute-start(f32[1,20,64,1280]{3,2,1,0:T(8,128)} %get-tuple-element.1225), channel_id=1, source_target_pairs={{0,1},{1,0},{2,3},{3,2},{4,5},{5,4},{6,7},{7,6}} | collective-permute-start | bytes 19660808 | tf_op jit(solution)/shard_map/while/body/eval_jaxpr/ppermute | solution.py:152
  1992.1 196.8 %collective-permute-start.8 = (f32[1,1280,5120]{2,1,0:T(8,128)}, f32[1,1280,5120]{2,1,0:T(8,128)}, u32[]{:S(2)}, u32[]{:S(2)}) collective-permute-start(f32[1,1280,5120]{2,1,0:T(8,128)} %get-tuple-element.1226), channel_id=1, source_target_pairs={{0,1},{1,0},{2,3},{3,2},{4,5},{5,4},{6,7},{7,6}} | collective-permute-start | bytes 78643208 | tf_op jit(solution)/shard_map/while/body/eval_jaxpr/ppermute | solution.py:152
  1992.2 196.7 %collective-permute-start.9 = (f32[1,5120,1280]{2,1,0:T(8,128)}, f32[1,5120,1280]{2,1,0:T(8,128)}, u32[]{:S(2)}, u32[]{:S(2)}) collective-permute-start(f32[1,5120,1280]{2,1,0:T(8,128)} %get-tuple-element.1227), channel_id=1, source_target_pairs={{0,1},{1,0},{2,3},{3,2},{4,5},{5,4},{6,7},{7,6}} | collective-permute-start | bytes 78643208 | tf_op jit(solution)/shard_map/while/body/eval_jaxpr/ppermute | solution.py:152
  1992.7 97.2 %collective-permute-start.13 = (bf16[1,1280,3840]{2,1,0:T(8,128)(2,1)}, bf16[1,1280,3840]{2,1,0:T(8,128)(2,1)}, u32[]{:S(2)}, u32[]{:S(2)}) collective-permute-start(bf16[1,1280,3840]{2,1,0:T(8,128)(2,1)} %get-tuple-element.1218), channel_id=1, source_target_pairs={{0,1},{1,0},{2,3},{3,2},{4,5},{5,4},{6,7},{7,6}} | collective-permute-start | bytes 29491208 | tf_op jit(solution)/shard_map/while/body/eval_jaxpr/ppermute | solution.py:151
  1992.7 96.8 %collective-permute-start.14 = (bf16[1,20,64,1280]{3,2,1,0:T(8,128)(2,1)}, bf16[1,20,64,1280]{3,2,1,0:T(8,128)(2,1)S(1)}, u32[]{:S(2)}, u32[]{:S(2)}) collective-permute-start(bf16[1,20,64,1280]{3,2,1,0:T(8,128)(2,1)} %get-tuple-element.1219), channel_id=1, source_target_pairs={{0,1},{1,0},{2,3},{3,2},{4,5},{5,4},{6,7},{7,6}} | collective-permute-start | bytes 9830408 | tf_op jit(solution)/shard_map/while/body/eval_jaxpr/ppermute | solution.py:151
  1993.2 93.9 %collective-permute-start.12 = (bf16[1,1280]{1,0:T(2,128)(2,1)}, bf16[1,1280]{1,0:T(2,128)(2,1)S(1)}, u32[]{:S(2)}, u32[]{:S(2)}) collective-permute-start(bf16[1,1280]{1,0:T(2,128)(2,1)} %get-tuple-element.1222), channel_id=1, source_target_pairs={{0,1},{1,0},{2,3},{3,2},{4,5},{5,4},{6,7},{7,6}} | collective-permute-start | bytes 7688 | tf_op jit(solution)/shard_map/while/body/eval_jaxpr/ppermute | solution.py:151
  2089.6 99.3 %collective-permute-start.6 = (f32[1,1280,3840]{2,1,0:T(8,128)}, f32[1,1280,3840]{2,1,0:T(8,128)}, u32[]{:S(2)}, u32[]{:S(2)}) collective-permute-start(f32[1,1280,3840]{2,1,0:T(8,128)} %get-tuple-element.1224), channel_id=1, source_target_pairs={{0,1},{1,0},{2,3},{3,2},{4,5},{5,4},{6,7},{7,6}} | collective-permute-start | bytes 58982408 | tf_op jit(solution)/shard_map/while/body/eval_jaxpr/ppermute | solution.py:152
  2089.9 66.2 %collective-permute-start.17 = (bf16[1,5120,1280]{2,1,0:T(8,128)(2,1)}, bf16[1,5120,1280]{2,1,0:T(8,128)(2,1)}, u32[]{:S(2)}, u32[]{:S(2)}) collective-permute-start(bf16[1,5120,1280]{2,1,0:T(8,128)(2,1)} %get-tuple-element.1221), channel_id=1, source_target_pairs={{0,1},{1,0},{2,3},{3,2},{4,5},{5,4},{6,7},{7,6}} | collective-permute-start | bytes 39321608 | tf_op jit(solution)/shard_map/while/body/eval_jaxpr/ppermute | solution.py:151
  2109.3 79.7 %collective-permute-start.7 = (f32[1,20,64,1280]{3,2,1,0:T(8,128)}, f32[1,20,64,1280]{3,2,1,0:T(8,128)}, u32[]{:S(2)}, u32[]{:S(2)}) collective-permute-start(f32[1,20,64,1280]{3,2,1,0:T(8,128)} %get-tuple-element.1225), channel_id=1, source_target_pairs={{0,1},{1,0},{2,3},{3,2},{4,5},{5,4},{6,7},{7,6}} | collective-permute-start | bytes 19660808 | tf_op jit(solution)/shard_map/while/body/eval_jaxpr/ppermute | solution.py:152
  (137 other events, 5196.6 us)
Sparse Core Ops, SparseCore 0:
  2711.0 1293.0 all-reduce.3
where the time goes:
time: 4070 us; the launch traced here: 4060 us
  waiting for transfers between devices  1710 us (42%)
  matrix products  834 us (20%)
  local copies, waits for them, and re-layouts  655 us (16%)
  starting transfers between devices  595 us (15%)
  other arithmetic  207 us (5%)
    psum x1, waiting for transfers between devices, device_pass(): grads = tuple((lax.psum(acc_part, 'data') for acc_part in held_acc))  1270 us
    ppermute x12, starting transfers between devices, bwd_body(): lax.ppermute(acc_part, 'pipe', bwd_perm)  589 us
    ppermute x12, waiting for transfers between devices, bwd_body(): lax.ppermute(w_part, 'pipe', bwd_perm)  321 us
    while x68, local copies, waits for them, and re-layouts  252 us
    dot_general x2, matrix products, layer_forward(): jnp.einsum('msf,fd->msd', gelu_out, w_down, preferred_element_type=jnp.fl...  130 us
    ppermute x12, waiting for transfers between devices, fwd_body(): lax.ppermute(w_part, 'pipe', fwd_perm)  113 us
    unnamed x86, local copies, waits for them, and re-layouts  113 us
    dot_general x4, matrix products, layer_forward(): jnp.einsum('msd,df->msf', normed_m, w_up, preferred_element_type=jnp.floa...  104 us
  transfers between devices with their start and end apart: 37, of which 15 were waited for; matrix products, arithmetic and copies ran while one was open for 2% of the time, Pallas kernels for 0%

commit v1 on v0

v1 whole, which is shorter than its diff:
```python
import functools
import jax
import jax.numpy as jnp
from jax import lax
from jax.experimental import pallas as pl
from jax.experimental.pallas import tpu as pltpu
from jax.sharding import PartitionSpec as P


NORM_EPS = 1e-5
BF = jnp.bfloat16
F32 = jnp.float32
SEQ = 64
HEAD = 64
CHUNK = 64
NN = (((1,), (0,)), ((), ()))
NT = (((1,), (1,)), ((), ()))
TN = (((0,), (0,)), ((), ()))


def dot(lhs, rhs, dims=NN):
    return lax.dot_general(lhs, rhs, dims, preferred_element_type=F32)


def norm_fwd(hid, gain):
    inv_rms = lax.rsqrt(jnp.mean(hid * hid, axis=-1, keepdims=True) + NORM_EPS)
    return (hid * inv_rms * gain).astype(BF)


def norm_bwd(d_normed, hid, gain):
    inv_rms = lax.rsqrt(jnp.mean(hid * hid, axis=-1, keepdims=True) + NORM_EPS)
    unit = hid * inv_rms
    d_unit = d_normed * gain
    d_hid = inv_rms * (d_unit - unit * jnp.mean(d_unit * unit, axis=-1, keepdims=True))
    return d_hid, jnp.sum(d_normed * unit, axis=0)


def half_erf(pre):
    return 0.5 + 0.5 * lax.erf(pre * 0.7071067811865476)


def gelu_grad(pre, cdf):
    return cdf + pre * (jnp.exp(-0.5 * pre * pre) * 0.3989422804014327)


def mlp_fwd_body(rows, x_ref, res_ref, up_ref, down_ref, out_ref, pre_ref, acc_ref):
    step = pl.program_id(0)
    tokens = x_ref.shape[0]

    @pl.when(step == 0)
    def _():
        acc_ref[...] = res_ref[...].astype(F32)

    for start in range(0, tokens, rows):
        sl = pl.ds(start, rows)
        pre = dot(x_ref[sl, :], up_ref[0])
        pre_ref[sl, :] = pre
        act = (pre * half_erf(pre)).astype(BF)
        acc_ref[sl, :] += dot(act, down_ref[0])

    @pl.when(step == pl.num_programs(0) - 1)
    def _():
        out_ref[...] = acc_ref[...].astype(BF)


def mlp_fwd(normed, res, w_up, w_down, layer, fb=512, rows=512):
    tokens, dim = normed.shape
    ffn = w_up.shape[2]
    return pl.pallas_call(
        functools.partial(mlp_fwd_body, rows),
        grid=(ffn // fb,),
        in_specs=[
            pl.BlockSpec((tokens, dim), lambda f: (0, 0)),
            pl.BlockSpec((tokens, dim), lambda f: (0, 0)),
            pl.BlockSpec((1, dim, fb), lambda f: (layer, 0, f)),
            pl.BlockSpec((1, fb, dim), lambda f: (layer, f, 0)),
        ],
        out_specs=[
            pl.BlockSpec((tokens, dim), lambda f: (0, 0)),
            pl.BlockSpec((tokens, fb), lambda f: (0, f)),
        ],
        out_shape=[jax.ShapeDtypeStruct((tokens, dim), BF), jax.ShapeDtypeStruct((tokens, ffn), F32)],
        scratch_shapes=[pltpu.VMEM((tokens, dim), F32)],
        compiler_params=pltpu.CompilerParams(vmem_limit_bytes=56 * 1024 * 1024),
        cost_estimate=pl.CostEstimate(flops=4 * tokens * dim * ffn, bytes_accessed=4 * dim * ffn + 4 * tokens * ffn, transcendentals=tokens * ffn),
        name='mlp_fwd',
    )(normed, res, w_up, w_down)


def mlp_bwd_body(rows, dt_ref, pre_ref, up_ref, down_ref, out_ref):
    step = pl.program_id(0)
    tokens = dt_ref.shape[0]

    @pl.when(step == 0)
    def _():
        out_ref[...] = jnp.zeros_like(out_ref)

    for start in range(0, tokens, rows):
        sl = pl.ds(start, rows)
        d_act = dot(dt_ref[sl, :], down_ref[0], NT)
        pre = pre_ref[sl, :]
        d_pre = (d_act * gelu_grad(pre, half_erf(pre))).astype(BF)
        out_ref[sl, :] += dot(d_pre, up_ref[0], NT)


def mlp_bwd(d_top, pre, w_up, w_down, layer, fb=512, rows=512):
    tokens, dim = d_top.shape
    ffn = w_up.shape[2]
    return pl.pallas_call(
        functools.partial(mlp_bwd_body, rows),
        grid=(ffn // fb,),
        in_specs=[
            pl.BlockSpec((tokens, dim), lambda f: (0, 0)),
            pl.BlockSpec((tokens, fb), lambda f: (0, f)),
            pl.BlockSpec((1, dim, fb), lambda f: (layer, 0, f)),
            pl.BlockSpec((1, fb, dim), lambda f: (layer, f, 0)),
        ],
        out_specs=pl.BlockSpec((tokens, dim), lambda f: (0, 0)),
        out_shape=jax.ShapeDtypeStruct((tokens, dim), F32),
        compiler_params=pltpu.CompilerParams(vmem_limit_bytes=56 * 1024 * 1024),
        cost_estimate=pl.CostEstimate(flops=4 * tokens * dim * ffn, bytes_accessed=4 * dim * ffn + 4 * tokens * ffn, transcendentals=tokens * ffn),
        name='mlp_bwd',
    )(d_top, pre, w_up, w_down)


PER_TILE = 8
CHIPS = 4


def chunk_table_body(per_dev, count_ref, chip_ref, first_ref, tbl_ref):
    half = CHIPS * per_dev
    for group in range(2):
        def place(i, used, group=group):
            src, k = i // per_dev, i % per_dev
            live = k * CHUNK < count_ref[(src ^ chip_ref[0]) * 2 + group]
            slot = jnp.where(live, used, half - 1 - (i - used))
            tbl_ref[group * half + slot] = (src * 2 + group) * per_dev + k
            return used + jnp.where(live, 1, 0)

        used = lax.fori_loop(0, half, place, 0)
        tbl_ref[2 * half + group] = (used + PER_TILE - 1) // PER_TILE
    tbl_ref[2 * half + 2] = first_ref[0]


def chunk_table(counts, chip, first, per_dev):
    smem = pl.BlockSpec(memory_space=pltpu.SMEM)
    return pl.pallas_call(
        functools.partial(chunk_table_body, per_dev),
        in_specs=[smem] * 3,
        out_specs=smem,
        out_shape=jax.ShapeDtypeStruct((2 * CHIPS * per_dev + 3,), jnp.int32),
        name='chunk_table',
    )(counts, chip, first)


def mlp_grad_body(sub, half, tbl_ref, *refs):
    nm_refs, low_refs, high_refs, far_refs = (refs[k * PER_TILE:(k + 1) * PER_TILE] for k in range(4))
    up_ref, down_ref, gup_ref, gdown_ref, nm_s, dt_s = refs[4 * PER_TILE:]
    tile = pl.program_id(1)
    fb = up_ref.shape[1]
    near = tbl_ref[2 * half]
    low = tbl_ref[2 * half + 2] == 1

    @pl.when(tile == 0)
    def _():
        gup_ref[...] = jnp.zeros_like(gup_ref)
        gdown_ref[...] = jnp.zeros_like(gdown_ref)

    def take(dst, srcs):
        for k in range(PER_TILE):
            dst[pl.ds(k * CHUNK, CHUNK), :] = srcs[k][...]

    @pl.when(tile < near + tbl_ref[2 * half + 1])
    def _():
        take(nm_s, nm_refs)

        @pl.when((tile < near) & low)
        def _():
            take(dt_s, low_refs)

        @pl.when((tile < near) & jnp.logical_not(low))
        def _():
            take(dt_s, high_refs)

        @pl.when(tile >= near)
        def _():
            take(dt_s, far_refs)

        for start in range(0, fb, sub):
            sl = pl.ds(start, sub)
            pre = dot(nm_s[...], up_ref[:, sl])
            d_act = dot(dt_s[...], down_ref[sl, :], NT)
            cdf = half_erf(pre)
            act = (pre * cdf).astype(BF)
            gdown_ref[sl, :] += dot(act, dt_s[...], TN)
            d_pre = (d_act * gelu_grad(pre, cdf)).astype(BF)
            gup_ref[:, sl] += dot(nm_s[...], d_pre, TN)


def mlp_grad(table, normed_all, near_low, near_high, far, w_up, w_down, fb=1024, sub=512):
    tokens, dim = normed_all.shape
    ffn = w_up.shape[1]
    half = tokens // CHUNK // 2
    per_dev = half // CHIPS
    tiles = tokens // (CHUNK * PER_TILE)

    def group_chunk(entry):
        return entry // (2 * per_dev) * per_dev + entry % per_dev

    def any_spec(k):
        def index(f, t, tbl):
            near = tbl[2 * half]
            offset = jnp.where(t < near, t * PER_TILE, half + (jnp.minimum(t, near + tbl[2 * half + 1] - 1) - near) * PER_TILE)
            return tbl[offset + k], 0

        return pl.BlockSpec((CHUNK, dim), index)

    def near_spec(k, flag):
        def index(f, t, tbl):
            entry = group_chunk(tbl[jnp.minimum(t, tbl[2 * half] - 1) * PER_TILE + k])
            return jnp.where(tbl[2 * half + 2] == flag, entry, 0), 0

        return pl.BlockSpec((CHUNK, dim), index)

    def far_spec(k):
        def index(f, t, tbl):
            step = jnp.clip(t - tbl[2 * half], 0, tbl[2 * half + 1] - 1)
            return group_chunk(tbl[half + step * PER_TILE + k]), 0

        return pl.BlockSpec((CHUNK, dim), index)

    ks = range(PER_TILE)
    grid_spec = pltpu.PrefetchScalarGridSpec(
        num_scalar_prefetch=1,
        grid=(ffn // fb, tiles),
        in_specs=[any_spec(k) for k in ks] + [near_spec(k, 1) for k in ks] + [near_spec(k, 0) for k in ks] + [far_spec(k) for k in ks] + [
            pl.BlockSpec((dim, fb), lambda f, t, tbl: (0, f)),
            pl.BlockSpec((fb, dim), lambda f, t, tbl: (f, 0)),
        ],
        out_specs=[
            pl.BlockSpec((dim, fb), lambda f, t, tbl: (0, f)),
            pl.BlockSpec((fb, dim), lambda f, t, tbl: (f, 0)),
        ],
        scratch_shapes=[pltpu.VMEM((CHUNK * PER_TILE, dim), BF), pltpu.VMEM((CHUNK * PER_TILE, dim), BF)],
    )
    operands = [arr for arr in (normed_all, near_low, near_high, far) for _ in ks]
    return pl.pallas_call(
        functools.partial(mlp_grad_body, sub, half),
        grid_spec=grid_spec,
        out_shape=[jax.ShapeDtypeStruct((dim, ffn), F32), jax.ShapeDtypeStruct((ffn, dim), F32)],
        compiler_params=pltpu.CompilerParams(vmem_limit_bytes=62 * 1024 * 1024),
        cost_estimate=pl.CostEstimate(flops=8 * tokens * dim * ffn, bytes_accessed=12 * dim * ffn + 20 * tokens * dim, transcendentals=2 * tokens * ffn),
        name='mlp_grad',
    )(table, *operands, w_up, w_down)


def pair_mask(len_lo, len_hi):
    row = lax.broadcasted_iota(jnp.int32, (2 * SEQ, 2 * SEQ), 0)
    col = lax.broadcasted_iota(jnp.int32, (2 * SEQ, 2 * SEQ), 1)
    limit = jnp.where(row < SEQ, len_lo, len_hi + SEQ)
    floor = jnp.where(row < SEQ, 0, SEQ)
    return (col <= row) & (col < limit) & (col >= floor)


def head_masks():
    lane = lax.broadcasted_iota(jnp.int32, (1, 2 * HEAD), 1)
    low = jnp.where(lane < HEAD, 1.0, 0.0)
    return low.astype(BF), (1.0 - low).astype(BF)


def pair_softmax(query, key, visible):
    scores = jnp.where(visible, dot(query, key, NT) * HEAD ** -0.5, -1e30)
    weights = jnp.exp(scores - jnp.max(scores, axis=-1, keepdims=True))
    return weights * (1.0 / jnp.sum(weights, axis=-1, keepdims=True))


def attn_fwd_body(dim, len_ref, qkv_ref, ctx_ref):
    step = pl.program_id(0)
    visible = pair_mask(len_ref[2 * step], len_ref[2 * step + 1])
    masks = head_masks()
    for start in range(0, dim, 2 * HEAD):
        query = qkv_ref[:, pl.ds(start, 2 * HEAD)]
        key = qkv_ref[:, pl.ds(dim + start, 2 * HEAD)]
        value = qkv_ref[:, pl.ds(2 * dim + start, 2 * HEAD)]
        total = None
        for mask in masks:
            probs = pair_softmax(query * mask, key, visible).astype(BF)
            part = dot(probs, value * mask)
            total = part if total is None else total + part
        ctx_ref[:, pl.ds(start, 2 * HEAD)] = total.astype(BF)


def attn_fwd(lens, qkv):
    tokens, dim = qkv.shape[0], qkv.shape[1] // 3
    grid_spec = pltpu.PrefetchScalarGridSpec(
        num_scalar_prefetch=1,
        grid=(tokens // (2 * SEQ),),
        in_specs=[pl.BlockSpec((2 * SEQ, 3 * dim), lambda s, lens: (s, 0))],
        out_specs=pl.BlockSpec((2 * SEQ, dim), lambda s, lens: (s, 0)),
    )
    return pl.pallas_call(
        functools.partial(attn_fwd_body, dim),
        grid_spec=grid_spec,
        out_shape=jax.ShapeDtypeStruct((tokens, dim), BF),
        cost_estimate=pl.CostEstimate(flops=16 * tokens * 128 * dim, bytes_accessed=8 * tokens * dim, transcendentals=tokens * 128 * 20),
        name='attn_fwd',
    )(lens, qkv)


def attn_bwd_body(dim, len_ref, qkv_ref, dctx_ref, dqkv_ref):
    step = pl.program_id(0)
    visible = pair_mask(len_ref[2 * step], len_ref[2 * step + 1])
    masks = head_masks()
    for start in range(0, dim, 2 * HEAD):
        query = qkv_ref[:, pl.ds(start, 2 * HEAD)]
        key = qkv_ref[:, pl.ds(dim + start, 2 * HEAD)]
        value = qkv_ref[:, pl.ds(2 * dim + start, 2 * HEAD)]
        d_ctx = dctx_ref[:, pl.ds(start, 2 * HEAD)]
        d_query = d_key = d_value = 0.0
        for mask in masks:
            query_m, d_ctx_m = query * mask, d_ctx * mask
            probs = pair_softmax(query_m, key, visible)
            d_probs = dot(d_ctx_m, value, NT)
            inner = jnp.sum(probs * d_probs, axis=-1, keepdims=True)
            d_scores = (probs * (d_probs - inner) * HEAD ** -0.5).astype(BF)
            d_value = d_value + dot(probs.astype(BF), d_ctx_m, TN)
            d_query = d_query + dot(d_scores, key * mask)
            d_key = d_key + dot(d_scores, query_m, TN)
        dqkv_ref[:, pl.ds(start, 2 * HEAD)] = d_query.astype(BF)
        dqkv_ref[:, pl.ds(dim + start, 2 * HEAD)] = d_key.astype(BF)
        dqkv_ref[:, pl.ds(2 * dim + start, 2 * HEAD)] = d_value.astype(BF)


def attn_bwd(lens, qkv, d_ctx):
    tokens, dim = d_ctx.shape
    grid_spec = pltpu.PrefetchScalarGridSpec(
        num_scalar_prefetch=1,
        grid=(tokens // (2 * SEQ),),
        in_specs=[
            pl.BlockSpec((2 * SEQ, 3 * dim), lambda s, lens: (s, 0)),
            pl.BlockSpec((2 * SEQ, dim), lambda s, lens: (s, 0)),
        ],
        out_specs=pl.BlockSpec((2 * SEQ, 3 * dim), lambda s, lens: (s, 0)),
    )
    return pl.pallas_call(
        functools.partial(attn_bwd_body, dim),
        grid_spec=grid_spec,
        out_shape=jax.ShapeDtypeStruct((tokens, 3 * dim), BF),
        cost_estimate=pl.CostEstimate(flops=40 * tokens * 128 * dim, bytes_accessed=14 * tokens * dim, transcendentals=tokens * 128 * 20),
        name='attn_bwd',
    )(lens, qkv, d_ctx)


def solution(mesh):
    row_spec = P(('data', 'pipe'))
    stage_spec = P('pipe')
    swap = [(0, 1), (1, 0)]

    def flip_data(arr, bit):
        return lax.ppermute(arr, 'data', [(src, src ^ bit) for src in range(mesh.shape['data'])])

    def device_pass(acts_in, cot_out, seq_lens, w_qkv, w_out, w_up, w_down, gain_attn, gain_mlp):
        pipe = lax.axis_index('pipe')
        chip = lax.axis_index('data')
        seqs, seq, dim = acts_in.shape
        tokens = seqs * seq
        first = pipe == 0

        def gather_pair(part):
            return lax.all_gather(part, 'pipe', axis=0, tiled=True)

        wq = gather_pair(w_qkv)
        wo = gather_pair(w_out.reshape(1, dim, dim))
        wu = gather_pair(w_up)
        wd = gather_pair(w_down)
        gains_own = jnp.stack([gain_attn, gain_mlp], axis=1)
        gains_other = lax.ppermute(gains_own, 'pipe', swap)
        gains = jnp.where(first, jnp.concatenate([gains_own, gains_other]), jnp.concatenate([gains_other, gains_own])).astype(F32)

        pos = jnp.arange(seq)
        valid = pos[None, :] < seq_lens[:, None]
        cot = jnp.where(valid[:, :, None], cot_out, jnp.zeros_like(cot_out)).reshape(tokens, dim)

        order = jnp.arange(seqs)
        first_rank = jnp.sum(jnp.where(order[None, :] < order[:, None], seq_lens[None, :], 0), axis=1)
        rank = jnp.where(valid, first_rank[:, None] + pos[None, :], -1).reshape(1, tokens)
        pick = (rank == jnp.arange(tokens)[:, None]).astype(BF)

        count = jnp.full((8, 128), jnp.sum(seq_lens), jnp.int32)
        pair_counts = jnp.stack([count, lax.ppermute(count, 'pipe', swap)])
        half_counts = jnp.stack([pair_counts, flip_data(pair_counts, 1)])
        counts = jnp.concatenate([half_counts, flip_data(half_counts, 2)])[:, :, 0, 0].reshape(-1)
        table = chunk_table(counts, chip.astype(jnp.int32)[None], first.astype(jnp.int32)[None], tokens // CHUNK)

        cot_packed = dot(pick, cot_out.reshape(tokens, dim)).astype(BF)
        cot_group = lax.all_gather(cot_packed, 'data').reshape(-1, dim)

        saved = []
        hid = acts_in.reshape(tokens, dim)
        for layer in range(2):
            hid_f = hid.astype(F32)
            normed_a = norm_fwd(hid_f, gains[layer, 0])
            qkv = dot(normed_a, wq[layer]).astype(BF)
            ctx = attn_fwd(seq_lens, qkv)
            mid = (hid_f + dot(ctx, wo[layer])).astype(BF)
            normed_m = norm_fwd(mid.astype(F32), gains[layer, 1])
            out, pre = mlp_fwd(normed_m, mid, wu, wd, layer)
            saved.append((hid, normed_a, qkv, ctx, mid, normed_m, pre))
            hid = out
        acts_out = jnp.where(valid[:, :, None], hid.reshape(acts_in.shape), jnp.zeros_like(acts_in))

        def home(lower, upper):
            recv = lax.ppermute(jnp.where(first, upper, lower), 'pipe', swap)
            return jnp.where(first, lower, upper), recv

        nm_own = dot(pick, jnp.where(first, saved[0][5], saved[1][5])).astype(BF)
        nm_send = dot(pick, jnp.where(first, saved[1][5], saved[0][5])).astype(BF)
        nm_pair = jnp.stack([nm_own, lax.ppermute(nm_send, 'pipe', swap)])
        normed_all = lax.all_gather(nm_pair, 'data').reshape(-1, dim)
        na_home = home(saved[0][1], saved[1][1])
        ctx_home = home(saved[0][3], saved[1][3])

        d_hid = cot.astype(F32)
        d_mids, d_qkvs, d_gains = [None, None], [None, None], [None, None]
        for layer in (1, 0):
            hid_in, normed_a, qkv, ctx, mid, normed_m, pre = saved[layer]
            d_top = d_hid.astype(BF)
            if layer == 0:
                d_packed = dot(pick, d_top).astype(BF)
                d_group = lax.all_gather(d_packed, 'data').reshape(-1, dim)
            d_normed_m = mlp_bwd(d_top, pre, wu, wd, layer)
            d_norm, gain_m = norm_bwd(d_normed_m, mid.astype(F32), gains[layer, 1])
            d_mid = d_hid + d_norm
            d_mids[layer] = d_mid.astype(BF)
            d_ctx = dot(d_mids[layer], wo[layer], NT).astype(BF)
            d_qkvs[layer] = attn_bwd(seq_lens, qkv, d_ctx)
            d_normed_a = dot(d_qkvs[layer], wq[layer], NT)
            d_norm, gain_a = norm_bwd(d_normed_a, hid_in.astype(F32), gains[layer, 0])
            d_hid = d_mid + d_norm
            d_gains[layer] = jnp.stack([gain_a, gain_m])

        mid_home = home(*d_mids)
        qkv_home = home(*d_qkvs)
        g_qkv = dot(na_home[0], qkv_home[0], TN) + dot(na_home[1], qkv_home[1], TN)
        g_out = dot(ctx_home[0], mid_home[0], TN) + dot(ctx_home[1], mid_home[1], TN)

        d_group, g_qkv, g_out = lax.optimization_barrier((d_group, g_qkv, g_out))
        g_qkv, g_out = lax.psum((g_qkv, g_out), 'data')

        d_recv = lax.ppermute(jnp.where(first, cot_group, d_group), 'pipe', swap)
        grad_up, grad_down = mlp_grad(table, normed_all, d_group, cot_group, d_recv, w_up[0], w_down[0])

        gain_own, gain_recv = home(*d_gains)
        g_gain = gain_own + gain_recv
        g_gain = g_gain + flip_data(g_gain, 1)
        g_gain = g_gain + flip_data(g_gain, 2)
        return (acts_out, g_qkv[None], g_out.reshape(w_out.shape), grad_up[None], grad_down[None], g_gain[:1], g_gain[1:])

    return jax.shard_map(device_pass, mesh=mesh, in_specs=(row_spec, row_spec, row_spec) + (stage_spec,) * 6, out_specs=(row_spec,) + (stage_spec,) * 6, check_vma=False)
```

time: 4070 us -> 1330 us (0.33)
  waiting for transfers between devices: 1710 us -> 227 us
  Pallas kernels: 0 us -> 800 us
  matrix products: 834 us -> 176 us
  local copies, waits for them, and re-layouts: 655 us -> 28.4 us
  starting transfers between devices: 595 us -> 7.24 us
  other arithmetic: 207 us -> 63.7 us
    psum x1, waiting for transfers between devices: 1270 us -> 0.02 us  [device_pass(): g_qkv, g_out = lax.psum((g_qkv, g_out), 'data')]
    pallas_call x0 -> x10, Pallas kernels: none -> 800 us  [the longest x1 485 us: mlp_grad(): pl.pallas_call(functools.partial(mlp_grad_body, sub, half), grid_spec=gri...]
    dot_general x44 -> x16, matrix products: 834 us -> 176 us  [dot(): return lax.dot_general(lhs, rhs, dims, preferred_element_type=F32)]
    ppermute x36 -> x13, starting transfers between devices: 595 us -> 6.93 us  [the longest x4 4.41 us: flip_data(): lax.ppermute(arr, 'data', [(src, src ^ bit) for src in range(mesh.shape['...]
    ppermute x36 -> x13, waiting for transfers between devices: 435 us -> 3.82 us  [the longest x4 3.79 us: flip_data(): lax.ppermute(arr, 'data', [(src, src ^ bit) for src in range(mesh.shape['...]
    while x68 -> x0, local copies, waits for them, and re-layouts: 252 us -> none
    all_gather x0 -> x7, waiting for transfers between devices: none -> 221 us  [the longest x1 146 us: device_pass(): normed_all = lax.all_gather(nm_pair, 'data').reshape(-1, dim)]
    reshape x6 -> x0, local copies, waits for them, and re-layouts: 130 us -> none  [the longest x4 86.7 us: layer_forward(): qkv_all.astype(jnp.bfloat16).reshape(n_micro, seq_size, 3, heads, head_dim)]
  transfers between devices with their start and end apart: 37 -> 21, of which waited for: 15 -> 7; matrix products, arithmetic and copies ran while one was open for 2% -> 13% of each run, Pallas kernels for 0% -> 46%
where the time goes in v1:
time: 1330 us; the launch traced here: 1320 us
  Pallas kernels  800 us (60%)
  waiting for transfers between devices  227 us (17%)
  matrix products  176 us (13%)
  other arithmetic  63.7 us (5%)
  local copies, waits for them, and re-layouts  28.4 us (2%)
  between operations  14.9 us (1%)
    pallas_call x1, Pallas kernels, mlp_grad(): pl.pallas_call(functools.partial(mlp_grad_body, sub, half), grid_spec=gri...  485 us
    dot_general x16, matrix products, dot(): return lax.dot_general(lhs, rhs, dims, preferred_element_type=F32)  176 us
    all_gather x1, waiting for transfers between devices, device_pass(): normed_all = lax.all_gather(nm_pair, 'data').reshape(-1, dim)  146 us
    pallas_call x2, Pallas kernels, attn_bwd(): pl.pallas_call(functools.partial(attn_bwd_body, dim), grid_spec=grid_spec...  90.6 us
    pallas_call x2, Pallas kernels, mlp_bwd(): pl.pallas_call(functools.partial(mlp_bwd_body, rows), grid=(ffn // fb,),...  79.4 us
    pallas_call x2, Pallas kernels, mlp_fwd(): pl.pallas_call(functools.partial(mlp_fwd_body, rows), grid=(ffn // fb,),...  74.8 us
    all_gather x4, waiting for transfers between devices, gather_pair(): return lax.all_gather(part, 'pipe', axis=0, tiled=True)  72.3 us
    pallas_call x2, Pallas kernels, attn_fwd(): pl.pallas_call(functools.partial(attn_fwd_body, dim), grid_spec=grid_spec...  67.4 us
  transfers between devices with their start and end apart: 21, of which 7 were waited for; matrix products, arithmetic and copies ran while one was open for 13% of the time, Pallas kernels for 46%

profile of v1, /device:TPU:0, one launch (start us, length us, event | category | flops | bytes accessed | tf_op | source)
XLA Modules:
  0.0 1317.3 jit_solution(4234792843904433372)
XLA Ops:
  15.4 28.6 %all-gather.11.cloned.1.call-done = bf16[2,1280,3840]{2,1,0:T(8,128)(2,1)} async-done(((bf16[1,1280,3840]{2,1,0:T(8,128)(2,1)}), bf16[2,1280,3840]{2,1,0:T(8,128)(2,1)}) %all-gather.11.cloned.1.call-update) | async-done | bytes 19660816 | tf_op jit(solution)/shard_map/all_gather | solution.py:370
  43.9 16.6 %fusion.12.qkv_ref = bf16[1024,3840]{1,0:T(8,128)(2,1)} fusion(bf16[1024,1280]{1,0:T(8,128)(2,1)} %bitcast.89, bf16[2,1280,3840]{2,1,0:T(8,128)(2,1)} %all-gather.11.cloned.1.call-done), kind=kOutput, calls=%fused_computation.21 | convolution fusion | flops 10070261760 | bytes 20316160 | tf_op jit(solution)/shard_map/dot_general | solution.py:22
  60.6 33.6 %attn_fwd.2 = bf16[1024,1280]{1,0:T(8,128)(2,1)} custom-call(s32[16]{0:T(128)} %len_ref.7, bf16[1024,3840]{1,0:T(8,128)(2,1)} %fusion.12.qkv_ref), custom_call_target="tpu_custom_call" | custom-call | flops 2684354560 | bytes 10485760 | tf_op jit(solution)/shard_map/attn_fwd/pallas_call | solution.py:301
  104.6 43.4 %all-gather.17.cloned.1.call-done.down_ref = bf16[2,5120,1280]{2,1,0:T(8,128)(2,1)} async-done(((bf16[1,5120,1280]{2,1,0:T(8,128)(2,1)}), bf16[2,5120,1280]{2,1,0:T(8,128)(2,1)}) %all-gather.17.cloned.1.call-update) | async-done | bytes 26214416 | tf_op jit(solution)/shard_map/all_gather | solution.py:370
  148.0 37.3 %mlp_fwd.2 = (bf16[1024,1280]{1,0:T(8,128)(2,1)}, f32[1024,5120]{1,0:T(8,128)}) custom-call(bf16[1024,1280]{1,0:T(8,128)(2,1)} %fusion.21.x_ref, bf16[1024,1280]{1,0:T(8,128)(2,1)} %copy-done.7, bf16[2,1280,5120]{2,1,0:T(8,128)(2,1)} %all-gather.15.cloned.1.call-done.up_ref, bf16[2,5120,1280]{2,1,0:T(8,128)(2,1)} %all-gather.17.cloned.1.call-done.down_ref), custom_call_target="tpu_custom_call" | custom-call | flops 26843545600 | bytes 47185920 | tf_op jit(solution)/shard_map/mlp_fwd/pallas_call | solution.py:69
  187.6 17.0 %fusion.11.qkv_ref = bf16[1024,3840]{1,0:T(8,128)(2,1)} fusion(bf16[2,1280,3840]{2,1,0:T(8,128)(2,1)} %all-gather.11.cloned.1.call-done, bf16[1024,1280]{1,0:T(8,128)(2,1)} %get-tuple-element.16, f32[1280]{0:T(1024)S(1)} %get-tuple-element.32, f32[1024]{0:T(1024)S(1)} %add_rsqrt_fusion.2), kind=kOutput, calls=%fused_computation.20 | convolution fusion | flops 10075504640 | bytes 20325376 | tf_op jit(solution)/shard_map/dot_general | solution.py:22
  204.6 33.8 %attn_fwd.3 = bf16[1024,1280]{1,0:T(8,128)(2,1)} custom-call(s32[16]{0:T(128)} %len_ref.7, bf16[1024,3840]{1,0:T(8,128)(2,1)} %fusion.11.qkv_ref), custom_call_target="tpu_custom_call" | custom-call | flops 2684354560 | bytes 10485760 | tf_op jit(solution)/shard_map/attn_fwd/pallas_call | solution.py:301
  247.3 37.5 %mlp_fwd.3 = (bf16[1024,1280]{1,0:T(8,128)(2,1)}, f32[1024,5120]{1,0:T(8,128)}) custom-call(bf16[1024,1280]{1,0:T(8,128)(2,1)} %fusion.29.x_ref, bf16[1024,1280]{1,0:T(8,128)(2,1)} %copy-done.9, bf16[2,1280,5120]{2,1,0:T(8,128)(2,1)} %all-gather.15.cloned.1.call-done.up_ref, bf16[2,5120,1280]{2,1,0:T(8,128)(2,1)} %all-gather.17.cloned.1.call-done.down_ref), custom_call_target="tpu_custom_call" | custom-call | flops 26843545600 | bytes 47185920 | tf_op jit(solution)/shard_map/mlp_fwd/pallas_call | solution.py:69
  288.7 39.4 %mlp_bwd.2 = f32[1024,1280]{1,0:T(8,128)} custom-call(bf16[1024,1280]{1,0:T(8,128)(2,1)} %bitcast.85, f32[1024,5120]{1,0:T(8,128)} %get-tuple-element.18.pre_ref, bf16[2,1280,5120]{2,1,0:T(8,128)(2,1)} %all-gather.15.cloned.1.call-done.up_ref, bf16[2,5120,1280]{2,1,0:T(8,128)(2,1)} %all-gather.17.cloned.1.call-done.down_ref), custom_call_target="tpu_custom_call" | custom-call | flops 26843545600 | bytes 47185920 | tf_op jit(solution)/shard_map/mlp_bwd/pallas_call | solution.py:109
  342.1 45.5 %attn_bwd.2 = bf16[1024,3840]{1,0:T(8,128)(2,1)} custom-call(s32[16]{0:T(128)} %len_ref.7, bf16[1024,3840]{1,0:T(8,128)(2,1)} %fusion.11.qkv_ref, bf16[1024,1280]{1,0:T(8,128)(2,1)} %convolution_convert_fusion.1.dctx_ref), custom_call_target="tpu_custom_call" | custom-call | flops 6710886400 | bytes 18350080 | tf_op jit(solution)/shard_map/attn_bwd/pallas_call | solution.py:345
  387.6 18.4 %fusion.41 = (f32[1280]{0:T(1024)}, f32[1024]{0:T(1024)S(1)}, f32[1024,1280]{1,0:T(8,128)}) fusion(bf16[1024,1280]{1,0:T(8,128)(2,1)} %get-tuple-element.16, f32[1024]{0:T(1024)S(1)} %add_rsqrt_fusion.2, f32[1280]{0:T(1024)S(1)} %get-tuple-element.32, bf16[1024,3840]{1,0:T(8,128)(2,1)} %attn_bwd.2, bf16[2,1280,3840]{2,1,0:T(8,128)(2,1)} %all-gather.11.cloned.1.call-done), kind=kOutput, calls=%fused_computation.54 | convolution fusion | flops 10075502592 | bytes 25577472 | tf_op jit(solution)/shard_map/dot_general | solution.py:22
  436.8 40.0 %mlp_bwd.3 = f32[1024,1280]{1,0:T(8,128)} custom-call(bf16[1024,1280]{1,0:T(8,128)(2,1)} %copy-done.21, f32[1024,5120]{1,0:T(8,128)} %get-tuple-element.19.pre_ref, bf16[2,1280,5120]{2,1,0:T(8,128)(2,1)} %all-gather.15.cloned.1.call-done.up_ref, bf16[2,5120,1280]{2,1,0:T(8,128)(2,1)} %all-gather.17.cloned.1.call-done.down_ref), custom_call_target="tpu_custom_call" | custom-call | flops 26843545600 | bytes 47185920 | tf_op jit(solution)/shard_map/mlp_bwd/pallas_call | solution.py:109
  482.4 9.0 broadcast_select_fusion.4
  491.5 7.8 convolution_convert_fusion.dctx_ref
  499.3 45.1 %attn_bwd.3 = bf16[1024,3840]{1,0:T(8,128)(2,1)} custom-call(s32[16]{0:T(128)} %len_ref.7, bf16[1024,3840]{1,0:T(8,128)(2,1)} %fusion.12.qkv_ref, bf16[1024,1280]{1,0:T(8,128)(2,1)} %convolution_convert_fusion.dctx_ref), custom_call_target="tpu_custom_call" | custom-call | flops 6710886400 | bytes 18350080 | tf_op jit(solution)/shard_map/attn_bwd/pallas_call | solution.py:345
  556.7 8.5 fusion.63
  565.2 18.3 %fusion.4 = f32[1280,3840]{1,0:T(8,128)} fusion(bf16[1024,3840]{1,0:T(8,128)(2,1)} %attn_bwd.3, bf16[1024,3840]{1,0:T(8,128)(2,1)} %attn_bwd.2, pred[]{:T(512)S(6)} %eq.16, bf16[1024,1280]{1,0:T(8,128)(2,1)S(1)} %copy-done.12, bf16[1024,1280]{1,0:T(8,128)(2,1)S(1)} %copy-done.3, f32[1280]{0:T(1024)S(1)} %get-tuple-element.32, f32[1024]{0:T(1024)S(1)} %add_rsqrt_fusion.2), kind=kOutput, calls=%fused_computation.9 | convolution fusion | flops 10076815360 | bytes 40641536 | tf_op jit(solution)/shard_map/dot_general | solution.py:22
  583.5 10.8 convolution_add_fusion.1
  594.4 21.0 %convolution_add_fusion = f32[1280,3840]{1,0:T(8,128)} fusion(f32[1280,3840]{1,0:T(8,128)} %fusion.4, bf16[1024,1280]{1,0:T(8,128)(2,1)} %collective-permute-done.1, bf16[1024,3840]{1,0:T(8,128)(2,1)} %collective-permute-done.2), kind=kOutput, calls=%fused_computation | convolution fusion | flops 10071244800 | bytes 49807360 | tf_op jit(solution)/shard_map/dot_general | solution.py:22
  617.7 10.4 broadcast_select_fusion
  630.0 17.5 %fusion.47 = f32[1280]{0:T(1024)S(1)} fusion(bf16[16,64,1280]{2,1,0:T(8,128)(2,1)S(1)} %copy-done.6, bf16[1024,3840]{1,0:T(8,128)(2,1)} %attn_bwd.3, bf16[2,1280,3840]{2,1,0:T(8,128)(2,1)} %all-gather.11.cloned.1.call-done, f32[1024]{0:T(1024)S(1)} %rsqrt.44), kind=kOutput, calls=%fused_computation.65 | convolution fusion | flops 10071571456 | bytes 20325376 | tf_op jit(solution)/shard_map/dot_general | solution.py:22
  661.2 146.4 %all-gather.21.cloned.1.call-done = bf16[8,1024,1280]{2,1,0:T(8,128)(2,1)} async-done(((bf16[2,1024,1280]{2,1,0:T(8,128)(2,1)}), bf16[8,1024,1280]{2,1,0:T(8,128)(2,1)}) %all-gather.21.cloned.1.call-update) | async-done | bytes 20971536 | tf_op jit(solution)/shard_map/all_gather | solution.py:419
  807.6 484.6 %mlp_grad.1 = (f32[1280,5120]{1,0:T(8,128)}, f32[5120,1280]{1,0:T(8,128)}) custom-call(s32[131]{0:T(256)} %chunk_table.1.tbl_ref, bf16[8192,1280]{1,0:T(8,128)(2,1)} %bitcast.99, bf16[8192,1280]{1,0:T(8,128)(2,1)} %bitcast.100, bf16[8192,1280]{1,0:T(8,128)(2,1)} %bitcast.101, bf16[8192,1280]{1,0:T(8,128)(2,1)} %bitcast.102, bf16[8192,1280]{1,0:T(8,128)(2,1)} %bitcast.103, ...), custom_call_target="tpu_custom_call" | custom-call | flops 429496729600 | bytes 288358400 | tf_op jit(solution)/shard_map/mlp_grad/pallas_call | solution.py:247
  1292.3 15.2 %copy.20 = f32[1,1280,3840]{2,1,0:T(8,128)} copy(f32[1,1280,3840]{2,1,0:T(8,128)} %get-tuple-element.55) | data formatting | bytes 39321600
  (188 shorter events, 116.5 us)
Async XLA Ops:
  7.2 36.8 %all-gather.11.cloned.1.call-start = ((), (), s32[]{:S(2)}) async-start(), calls=%async_computation | async-start | bytes 29491200 | tf_op jit(solution)/shard_map/all_gather | solution.py:370
  7.9 86.3 %all-gather.13.cloned.1.call-start = ((), (), s32[]{:S(2)}) async-start(), calls=%async_computation.1 | async-start | bytes 9830400 | tf_op jit(solution)/shard_map/all_gather | solution.py:370
  8.7 95.9 %all-gather.15.cloned.1.call-start = ((), (), s32[]{:S(2)}) async-start(), calls=%async_computation.2 | async-start | bytes 39321600 | tf_op jit(solution)/shard_map/all_gather | solution.py:370
  9.4 138.5 %all-gather.17.cloned.1.call-start = ((), (), s32[]{:S(2)}) async-start(), calls=%async_computation.3 | async-start | bytes 39321600 | tf_op jit(solution)/shard_map/all_gather | solution.py:370
  10.0 605.4 %all-gather.19.cloned.1.call-start = ((), (), s32[]{:S(2)}) async-start(), calls=%async_computation.4 | async-start | bytes 13107200 | tf_op jit(solution)/shard_map/all_gather | solution.py:430
  10.1 2.4 collective-permute-start
  11.8 48.8 %copy-start.26 = (f32[16,64]{1,0:T(8,128)}, f32[16,64]{1,0:T(8,128)S(1)}, u32[]{:S(2)}) copy-start(f32[16,64]{1,0:T(8,128)S(1)} %add_rsqrt_fusion) | copy-start | bytes 12292
  12.6 88.1 %copy-start.22 = (f32[1280]{0:T(1024)}, f32[1280]{0:T(1024)S(1)}, u32[]{:S(2)}) copy-start(f32[1280]{0:T(1024)S(1)} %get-tuple-element.33) | copy-start | bytes 15364
  342.1 63.9 %slice-start = ((s8[5242880]{0:T(1024)(128)(4,1)}), s8[1048576]{0:T(1024)(128)(4,1)S(1)}, s32[]{:S(2)}) async-start(s8[5242880]{0:T(1024)(128)(4,1)} %bitcast.78), calls=%async_computation.8 | async-start | bytes 2097152
  415.9 201.8 %all-gather.23.cloned.1.call-start = ((), (), s32[]{:S(2)}) async-start(), calls=%async_computation.6 | async-start | bytes 13107200 | tf_op jit(solution)/shard_map/all_gather | solution.py:396
  422.2 385.4 %all-gather.21.cloned.1.call-start = ((), (), s32[]{:S(2)}) async-start(), calls=%async_computation.5 | async-start | bytes 26214400 | tf_op jit(solution)/shard_map/all_gather | solution.py:419
  428.8 5.1 collective-permute-start.8
  436.7 855.5 %all-reduce.4.cloned.1.call-start = ((), (), s32[]{:S(2)}) async-start(), calls=%async_computation.7 | async-start | bytes 52428800 | tf_op jit(solution)/shard_map/psum | solution.py:448
  551.8 42.5 %collective-permute-start.2 = (bf16[1024,3840]{1,0:T(8,128)(2,1)}, bf16[1024,3840]{1,0:T(8,128)(2,1)}, u32[]{:S(2)}, u32[]{:S(2)}) collective-permute-start(bf16[1024,3840]{1,0:T(8,128)(2,1)} %broadcast_select_fusion.1), channel_id=1, source_target_pairs={{0,1},{1,0},{2,3},{3,2},{4,5},{5,4},{6,7},{7,6}} | collective-permute-start | bytes 23592968 | tf_op jit(solution)/shard_map/ppermute | solution.py:413
  556.1 27.4 %collective-permute-start.3 = (bf16[1024,1280]{1,0:T(8,128)(2,1)}, bf16[1024,1280]{1,0:T(8,128)(2,1)}, u32[]{:S(2)}, u32[]{:S(2)}) collective-permute-start(bf16[1024,1280]{1,0:T(8,128)(2,1)} %broadcast_select_fusion.3), channel_id=1, source_target_pairs={{0,1},{1,0},{2,3},{3,2},{4,5},{5,4},{6,7},{7,6}} | collective-permute-start | bytes 7864328 | tf_op jit(solution)/shard_map/ppermute | solution.py:413
  556.1 27.4 %collective-permute-start.4 = (bf16[1024,1280]{1,0:T(8,128)(2,1)}, bf16[1024,1280]{1,0:T(8,128)(2,1)}, u32[]{:S(2)}, u32[]{:S(2)}) collective-permute-start(bf16[1024,1280]{1,0:T(8,128)(2,1)} %get-tuple-element.41), channel_id=1, source_target_pairs={{0,1},{1,0},{2,3},{3,2},{4,5},{5,4},{6,7},{7,6}} | collective-permute-start | bytes 7864328 | tf_op jit(solution)/shard_map/ppermute | solution.py:413
  556.6 37.8 %collective-permute-start.1 = (bf16[1024,1280]{1,0:T(8,128)(2,1)}, bf16[1024,1280]{1,0:T(8,128)(2,1)}, u32[]{:S(2)}, u32[]{:S(2)}) collective-permute-start(bf16[1024,1280]{1,0:T(8,128)(2,1)} %get-tuple-element.39), channel_id=1, source_target_pairs={{0,1},{1,0},{2,3},{3,2},{4,5},{5,4},{6,7},{7,6}} | collective-permute-start | bytes 7864328 | tf_op jit(solution)/shard_map/ppermute | solution.py:413
  628.1 33.0 %collective-permute-start.9 = (bf16[4096,1280]{1,0:T(8,128)(2,1)}, bf16[4096,1280]{1,0:T(8,128)(2,1)}, u32[]{:S(2)}, u32[]{:S(2)}) collective-permute-start(bf16[4096,1280]{1,0:T(8,128)(2,1)} %broadcast_select_fusion), channel_id=1, source_target_pairs={{0,1},{1,0},{2,3},{3,2},{4,5},{5,4},{6,7},{7,6}} | collective-permute-start | bytes 31457288 | tf_op jit(solution)/shard_map/ppermute | solution.py:450
  629.4 18.2 %collective-permute-start.5 = (s32[8,128]{1,0:T(8,128)S(1)}, s32[8,128]{1,0:T(8,128)S(1)}, u32[]{:S(2)}, u32[]{:S(2)}) collective-permute-start(s32[8,128]{1,0:T(8,128)S(1)} %broadcast_in_dim.73), channel_id=1, source_target_pairs={{0,1},{1,0},{2,3},{3,2},{4,5},{5,4},{6,7},{7,6}} | collective-permute-start | bytes 12296 | tf_op jit(solution)/shard_map/ppermute | solution.py:390
  647.5 2.2 collective-permute-start.10
  648.3 4.0 collective-permute-start.6
  649.7 4.0 collective-permute-start.11
  652.3 4.3 collective-permute-start.7
  653.8 6.7 collective-permute-start.12
  (40 other events, 487.0 us)
Sparse Core Ops, SparseCore 0:
  9.5 34.4 all-gather.10
  45.5 15.5 all-gather.12
  62.6 41.9 all-gather.14
  106.0 41.9 all-gather.16
  416.0 100.5 all-gather.18
  518.2 99.3 all-gather.22
  619.5 188.0 all-gather.20
  811.9 448.9 all-reduce.3

commit v2 on v1

--- a/solution.py
+++ b/solution.py
@@ -43,7 +43,7 @@
     return cdf + pre * (jnp.exp(-0.5 * pre * pre) * 0.3989422804014327)
 
 
-def mlp_fwd_body(rows, x_ref, res_ref, up_ref, down_ref, out_ref, pre_ref, acc_ref):
+def mlp_fwd_body(rows, own_ref, x_ref, res_ref, own_up_ref, own_down_ref, far_up_ref, far_down_ref, out_ref, pre_ref, acc_ref):
     step = pl.program_id(0)
     tokens = x_ref.shape[0]
 
@@ -51,43 +51,57 @@
     def _():
         acc_ref[...] = res_ref[...].astype(F32)
 
-    for start in range(0, tokens, rows):
-        sl = pl.ds(start, rows)
-        pre = dot(x_ref[sl, :], up_ref[0])
-        pre_ref[sl, :] = pre
-        act = (pre * half_erf(pre)).astype(BF)
-        acc_ref[sl, :] += dot(act, down_ref[0])
+    def run(up_ref, down_ref):
+        for start in range(0, tokens, rows):
+            sl = pl.ds(start, rows)
+            pre = dot(x_ref[sl, :], up_ref[0])
+            pre_ref[sl, :] = pre
+            act = (pre * half_erf(pre)).astype(BF)
+            acc_ref[sl, :] += dot(act, down_ref[0])
+
+    @pl.when(own_ref[0] == 1)
+    def _():
+        run(own_up_ref, own_down_ref)
+
+    @pl.when(own_ref[0] == 0)
+    def _():
+        run(far_up_ref, far_down_ref)
 
     @pl.when(step == pl.num_programs(0) - 1)
     def _():
         out_ref[...] = acc_ref[...].astype(BF)
 
 
-def mlp_fwd(normed, res, w_up, w_down, layer, fb=512, rows=512):
+def weight_specs(dim, fb):
+    return [
+        pl.BlockSpec((1, dim, fb), lambda f, own: (0, 0, f * own[0])),
+        pl.BlockSpec((1, fb, dim), lambda f, own: (0, f * own[0], 0)),
+        pl.BlockSpec((1, dim, fb), lambda f, own: (0, 0, f * (1 - own[0]))),
+        pl.BlockSpec((1, fb, dim), lambda f, own: (0, f * (1 - own[0]), 0)),
+    ]
+
+
+def mlp_fwd(own, normed, res, weights, fb=512, rows=512):
     tokens, dim = normed.shape
-    ffn = w_up.shape[2]
+    ffn = weights[0].shape[2]
+    whole = pl.BlockSpec((tokens, dim), lambda f, own: (0, 0))
     return pl.pallas_call(
         functools.partial(mlp_fwd_body, rows),
-        grid=(ffn // fb,),
-        in_specs=[
-            pl.BlockSpec((tokens, dim), lambda f: (0, 0)),
-            pl.BlockSpec((tokens, dim), lambda f: (0, 0)),
-            pl.BlockSpec((1, dim, fb), lambda f: (layer, 0, f)),
-            pl.BlockSpec((1, fb, dim), lambda f: (layer, f, 0)),
-        ],
-        out_specs=[
-            pl.BlockSpec((tokens, dim), lambda f: (0, 0)),
-            pl.BlockSpec((tokens, fb), lambda f: (0, f)),
-        ],
+        grid_spec=pltpu.PrefetchScalarGridSpec(
+            num_scalar_prefetch=1,
+            grid=(ffn // fb,),
+            in_specs=[whole, whole] + weight_specs(dim, fb),
+            out_specs=[whole, pl.BlockSpec((tokens, fb), lambda f, own: (0, f))],
+            scratch_shapes=[pltpu.VMEM((tokens, dim), F32)],
+        ),
         out_shape=[jax.ShapeDtypeStruct((tokens, dim), BF), jax.ShapeDtypeStruct((tokens, ffn), F32)],
-        scratch_shapes=[pltpu.VMEM((tokens, dim), F32)],
         compiler_params=pltpu.CompilerParams(vmem_limit_bytes=56 * 1024 * 1024),
         cost_estimate=pl.CostEstimate(flops=4 * tokens * dim * ffn, bytes_accessed=4 * dim * ffn + 4 * tokens * ffn, transcendentals=tokens * ffn),
         name='mlp_fwd',
-    )(normed, res, w_up, w_down)
-
-
-def mlp_bwd_body(rows, dt_ref, pre_ref, up_ref, down_ref, out_ref):
+    )(own, normed, res, *weights)
+
+
+def mlp_bwd_body(rows, own_ref, dt_ref, pre_ref, own_up_ref, own_down_ref, far_up_ref, far_down_ref, out_ref):
     step = pl.program_id(0)
     tokens = dt_ref.shape[0]
 
@@ -95,32 +109,40 @@
     def _():
         out_ref[...] = jnp.zeros_like(out_ref)
 
-    for start in range(0, tokens, rows):
-        sl = pl.ds(start, rows)
-        d_act = dot(dt_ref[sl, :], down_ref[0], NT)
-        pre = pre_ref[sl, :]
-        d_pre = (d_act * gelu_grad(pre, half_erf(pre))).astype(BF)
-        out_ref[sl, :] += dot(d_pre, up_ref[0], NT)
-
-
-def mlp_bwd(d_top, pre, w_up, w_down, layer, fb=512, rows=512):
+    def run(up_ref, down_ref):
+        for start in range(0, tokens, rows):
+            sl = pl.ds(start, rows)
+            d_act = dot(dt_ref[sl, :], down_ref[0], NT)
+            pre = pre_ref[sl, :]
+            d_pre = (d_act * gelu_grad(pre, half_erf(pre))).astype(BF)
+            out_ref[sl, :] += dot(d_pre, up_ref[0], NT)
+
+    @pl.when(own_ref[0] == 1)
+    def _():
+        run(own_up_ref, own_down_ref)
+
+    @pl.when(own_ref[0] == 0)
+    def _():
+        run(far_up_ref, far_down_ref)
+
+
+def mlp_bwd(own, d_top, pre, weights, fb=512, rows=512):
     tokens, dim = d_top.shape
-    ffn = w_up.shape[2]
+    ffn = weights[0].shape[2]
+    whole = pl.BlockSpec((tokens, dim), lambda f, own: (0, 0))
     return pl.pallas_call(
         functools.partial(mlp_bwd_body, rows),
-        grid=(ffn // fb,),
-        in_specs=[
-            pl.BlockSpec((tokens, dim), lambda f: (0, 0)),
-            pl.BlockSpec((tokens, fb), lambda f: (0, f)),
-            pl.BlockSpec((1, dim, fb), lambda f: (layer, 0, f)),
-            pl.BlockSpec((1, fb, dim), lambda f: (layer, f, 0)),
-        ],
-        out_specs=pl.BlockSpec((tokens, dim), lambda f: (0, 0)),
+        grid_spec=pltpu.PrefetchScalarGridSpec(
+            num_scalar_prefetch=1,
+            grid=(ffn // fb,),
+            in_specs=[whole, pl.BlockSpec((tokens, fb), lambda f, own: (0, f))] + weight_specs(dim, fb),
+            out_specs=whole,
+        ),
         out_shape=jax.ShapeDtypeStruct((tokens, dim), F32),
         compiler_params=pltpu.CompilerParams(vmem_limit_bytes=56 * 1024 * 1024),
         cost_estimate=pl.CostEstimate(flops=4 * tokens * dim * ffn, bytes_accessed=4 * dim * ffn + 4 * tokens * ffn, transcendentals=tokens * ffn),
         name='mlp_bwd',
-    )(d_top, pre, w_up, w_down)
+    )(own, d_top, pre, *weights)
 
 
 PER_TILE = 8
@@ -197,7 +219,7 @@
             gup_ref[:, sl] += dot(nm_s[...], d_pre, TN)
 
 
-def mlp_grad(table, normed_all, near_low, near_high, far, w_up, w_down, fb=1024, sub=512):
+def mlp_grad(table, normed_all, near_low, near_high, far, w_up, w_down, fb=1280, sub=1280):
     tokens, dim = normed_all.shape
     ffn = w_up.shape[1]
     half = tokens // CHUNK // 2
@@ -371,8 +393,8 @@
 
         wq = gather_pair(w_qkv)
         wo = gather_pair(w_out.reshape(1, dim, dim))
-        wu = gather_pair(w_up)
-        wd = gather_pair(w_down)
+        mlp_weights = (w_up, w_down, lax.ppermute(w_up, 'pipe', swap), lax.ppermute(w_down, 'pipe', swap))
+        owned = [(pipe == layer).astype(jnp.int32)[None] for layer in range(2)]
         gains_own = jnp.stack([gain_attn, gain_mlp], axis=1)
         gains_other = lax.ppermute(gains_own, 'pipe', swap)
         gains = jnp.where(first, jnp.concatenate([gains_own, gains_other]), jnp.concatenate([gains_other, gains_own])).astype(F32)
@@ -404,9 +426,11 @@
             ctx = attn_fwd(seq_lens, qkv)
             mid = (hid_f + dot(ctx, wo[layer])).astype(BF)
             normed_m = norm_fwd(mid.astype(F32), gains[layer, 1])
-            out, pre = mlp_fwd(normed_m, mid, wu, wd, layer)
+            out, pre = mlp_fwd(owned[layer], normed_m, mid, mlp_weights)
             saved.append((hid, normed_a, qkv, ctx, mid, normed_m, pre))
             hid = out
+            if layer == 0:
+                hid, table = lax.optimization_barrier((hid, table))
         acts_out = jnp.where(valid[:, :, None], hid.reshape(acts_in.shape), jnp.zeros_like(acts_in))
 
         def home(lower, upper):
@@ -428,7 +452,7 @@
             if layer == 0:
                 d_packed = dot(pick, d_top).astype(BF)
                 d_group = lax.all_gather(d_packed, 'data').reshape(-1, dim)
-            d_normed_m = mlp_bwd(d_top, pre, wu, wd, layer)
+            d_normed_m = mlp_bwd(owned[layer], d_top, pre, mlp_weights)
             d_norm, gain_m = norm_bwd(d_normed_m, mid.astype(F32), gains[layer, 1])
             d_mid = d_hid + d_norm
             d_mids[layer] = d_mid.astype(BF)

time: 1330 us -> 1290 us (0.970)
  Pallas kernels: 800 us -> 781 us
  waiting for transfers between devices: 227 us -> 208 us
    all_gather x4 -> x2, waiting for transfers between devices: 72.3 us -> 0.02 us  [gather_pair(): return lax.all_gather(part, 'pipe', axis=0, tiled=True)]
    ppermute x1, waiting for transfers between devices: 0.01 us -> 49 us  [device_pass(): pair_counts = jnp.stack([count, lax.ppermute(count, 'pipe', swap)])]
    pallas_call x1, Pallas kernels: 485 us -> 461 us  [mlp_grad(): pl.pallas_call(functools.partial(mlp_grad_body, sub, half), grid_spec=gri...]
  transfers between devices with their start and end apart: 21 -> 21, of which waited for: 7 -> 6; matrix products, arithmetic and copies ran while one was open for 13% -> 14% of each run, Pallas kernels for 46% -> 45%
where the time goes in v2:
time: 1290 us; the launch traced here: 1280 us
  Pallas kernels  781 us (61%)
  waiting for transfers between devices  208 us (16%)
  matrix products  177 us (14%)
  other arithmetic  64.2 us (5%)
  local copies, waits for them, and re-layouts  26.2 us (2%)
  between operations  15.2 us (1%)
    pallas_call x1, Pallas kernels, mlp_grad(): pl.pallas_call(functools.partial(mlp_grad_body, sub, half), grid_spec=gri...  461 us
    dot_general x16, matrix products, dot(): return lax.dot_general(lhs, rhs, dims, preferred_element_type=F32)  177 us
    all_gather x1, waiting for transfers between devices, device_pass(): normed_all = lax.all_gather(nm_pair, 'data').reshape(-1, dim)  150 us
    pallas_call x2, Pallas kernels, attn_bwd(): pl.pallas_call(functools.partial(attn_bwd_body, dim), grid_spec=grid_spec...  90.3 us
    pallas_call x2, Pallas kernels, mlp_bwd(): pl.pallas_call(functools.partial(mlp_bwd_body, rows), grid_spec=pltpu.Pre...  81.6 us
    pallas_call x2, Pallas kernels, mlp_fwd(): pl.pallas_call(functools.partial(mlp_fwd_body, rows), grid_spec=pltpu.Pre...  77.8 us
    pallas_call x2, Pallas kernels, attn_fwd(): pl.pallas_call(functools.partial(attn_fwd_body, dim), grid_spec=grid_spec...  67.8 us
    ppermute x1, waiting for transfers between devices, device_pass(): pair_counts = jnp.stack([count, lax.ppermute(count, 'pipe', swap)])  49 us
  transfers between devices with their start and end apart: 21, of which 6 were waited for; matrix products, arithmetic and copies ran while one was open for 14% of the time, Pallas kernels for 45%

profile of v2, /device:TPU:0, one launch (start us, length us, event | category | flops | bytes accessed | tf_op | source)
XLA Modules:
  0.0 1283.5 jit_solution(20417570910643460)
XLA Ops:
  12.5 49.0 %collective-permute-done.3 = s32[8,128]{1,0:T(8,128)S(1)} collective-permute-done((s32[8,128]{1,0:T(8,128)S(1)}, s32[8,128]{1,0:T(8,128)S(1)}, u32[]{:S(2)}, u32[]{:S(2)}) %collective-permute-start.3) | collective-permute-done | bytes 4128 | tf_op jit(solution)/shard_map/ppermute | solution.py:412
  74.9 16.6 %fusion.12.qkv_ref = bf16[1024,3840]{1,0:T(8,128)(2,1)} fusion(bf16[1024,1280]{1,0:T(8,128)(2,1)} %bitcast.88, bf16[2,1280,3840]{2,1,0:T(8,128)(2,1)} %all-gather.9.cloned.1.call-done), kind=kOutput, calls=%fused_computation.21 | convolution fusion | flops 10070261760 | bytes 20316160 | tf_op jit(solution)/shard_map/dot_general | solution.py:22
  91.5 33.6 %attn_fwd.2 = bf16[1024,1280]{1,0:T(8,128)(2,1)} custom-call(s32[16]{0:T(128)} %len_ref.7, bf16[1024,3840]{1,0:T(8,128)(2,1)} %fusion.12.qkv_ref), custom_call_target="tpu_custom_call" | custom-call | flops 2684354560 | bytes 10485760 | tf_op jit(solution)/shard_map/attn_fwd/pallas_call | solution.py:323
  134.1 39.2 %mlp_fwd.2 = (bf16[1024,1280]{1,0:T(8,128)(2,1)}, f32[1024,5120]{1,0:T(8,128)}) custom-call(s32[1]{0:T(128)} %bitcast.1.own_ref.first_ref, bf16[1024,1280]{1,0:T(8,128)(2,1)} %fusion.21.x_ref, bf16[1024,1280]{1,0:T(8,128)(2,1)} %copy-done.7, bf16[1,1280,5120]{2,1,0:T(8,128)(2,1)} %own_up_ref.7, bf16[1,5120,1280]{2,1,0:T(8,128)(2,1)} %own_down_ref.7, ...), custom_call_target="tpu_custom_call" | custom-call | flops 26843545600 | bytes 47185920 | tf_op jit(solution)/shard_map/mlp_fwd/pallas_call | solution.py:88
  175.6 17.0 %fusion.11.qkv_ref = bf16[1024,3840]{1,0:T(8,128)(2,1)} fusion(bf16[2,1280,3840]{2,1,0:T(8,128)(2,1)} %all-gather.9.cloned.1.call-done, bf16[1024,1280]{1,0:T(8,128)(2,1)} %get-tuple-element.19, f32[1280]{0:T(1024)S(1)} %get-tuple-element.36, f32[1024]{0:T(1024)S(1)} %add_rsqrt_fusion.2), kind=kOutput, calls=%fused_computation.20 | convolution fusion | flops 10075504640 | bytes 20325376 | tf_op jit(solution)/shard_map/dot_general | solution.py:22
  192.6 34.2 %attn_fwd.3 = bf16[1024,1280]{1,0:T(8,128)(2,1)} custom-call(s32[16]{0:T(128)} %len_ref.7, bf16[1024,3840]{1,0:T(8,128)(2,1)} %fusion.11.qkv_ref), custom_call_target="tpu_custom_call" | custom-call | flops 2684354560 | bytes 10485760 | tf_op jit(solution)/shard_map/attn_fwd/pallas_call | solution.py:323
  235.5 38.6 %mlp_fwd.3 = (bf16[1024,1280]{1,0:T(8,128)(2,1)}, f32[1024,5120]{1,0:T(8,128)}) custom-call(s32[1]{0:T(128)} %bitcast.own_ref, bf16[1024,1280]{1,0:T(8,128)(2,1)} %fusion.29.x_ref, bf16[1024,1280]{1,0:T(8,128)(2,1)} %copy-done.9, bf16[1,1280,5120]{2,1,0:T(8,128)(2,1)} %own_up_ref.7, bf16[1,5120,1280]{2,1,0:T(8,128)(2,1)} %own_down_ref.7, ...), custom_call_target="tpu_custom_call" | custom-call | flops 26843545600 | bytes 47185920 | tf_op jit(solution)/shard_map/mlp_fwd/pallas_call | solution.py:88
  278.1 40.9 %mlp_bwd.2 = f32[1024,1280]{1,0:T(8,128)} custom-call(s32[1]{0:T(128)} %bitcast.own_ref, bf16[1024,1280]{1,0:T(8,128)(2,1)} %bitcast.84, f32[1024,5120]{1,0:T(8,128)} %get-tuple-element.21.pre_ref, bf16[1,1280,5120]{2,1,0:T(8,128)(2,1)} %own_up_ref.7, bf16[1,5120,1280]{2,1,0:T(8,128)(2,1)} %own_down_ref.7, ...), custom_call_target="tpu_custom_call" | custom-call | flops 26843545600 | bytes 47185920 | tf_op jit(solution)/shard_map/mlp_bwd/pallas_call | solution.py:133
  332.9 45.2 %attn_bwd.2 = bf16[1024,3840]{1,0:T(8,128)(2,1)} custom-call(s32[16]{0:T(128)} %len_ref.7, bf16[1024,3840]{1,0:T(8,128)(2,1)} %fusion.11.qkv_ref, bf16[1024,1280]{1,0:T(8,128)(2,1)} %convolution_convert_fusion.1.dctx_ref), custom_call_target="tpu_custom_call" | custom-call | flops 6710886400 | bytes 18350080 | tf_op jit(solution)/shard_map/attn_bwd/pallas_call | solution.py:367
  378.1 18.4 %fusion.41 = (f32[1280]{0:T(1024)}, f32[1024]{0:T(1024)S(1)}, f32[1024,1280]{1,0:T(8,128)}) fusion(bf16[1024,1280]{1,0:T(8,128)(2,1)} %get-tuple-element.19, f32[1024]{0:T(1024)S(1)} %add_rsqrt_fusion.2, f32[1280]{0:T(1024)S(1)} %get-tuple-element.36, bf16[1024,3840]{1,0:T(8,128)(2,1)} %attn_bwd.2, bf16[2,1280,3840]{2,1,0:T(8,128)(2,1)} %all-gather.9.cloned.1.call-done), kind=kOutput, calls=%fused_computation.54 | convolution fusion | flops 10075502592 | bytes 25577472 | tf_op jit(solution)/shard_map/dot_general | solution.py:22
  427.8 40.7 %mlp_bwd.3 = f32[1024,1280]{1,0:T(8,128)} custom-call(s32[1]{0:T(128)} %bitcast.1.own_ref.first_ref, bf16[1024,1280]{1,0:T(8,128)(2,1)} %copy-done.21, f32[1024,5120]{1,0:T(8,128)} %get-tuple-element.22.pre_ref, bf16[1,1280,5120]{2,1,0:T(8,128)(2,1)} %own_up_ref.7, bf16[1,5120,1280]{2,1,0:T(8,128)(2,1)} %own_down_ref.7, ...), custom_call_target="tpu_custom_call" | custom-call | flops 26843545600 | bytes 47185920 | tf_op jit(solution)/shard_map/mlp_bwd/pallas_call | solution.py:133
  474.1 9.0 broadcast_select_fusion.4
  483.1 7.8 convolution_convert_fusion.dctx_ref
  490.9 45.1 %attn_bwd.3 = bf16[1024,3840]{1,0:T(8,128)(2,1)} custom-call(s32[16]{0:T(128)} %len_ref.7, bf16[1024,3840]{1,0:T(8,128)(2,1)} %fusion.12.qkv_ref, bf16[1024,1280]{1,0:T(8,128)(2,1)} %convolution_convert_fusion.dctx_ref), custom_call_target="tpu_custom_call" | custom-call | flops 6710886400 | bytes 18350080 | tf_op jit(solution)/shard_map/attn_bwd/pallas_call | solution.py:367
  536.0 7.4 broadcast_select_fusion.1
  548.2 9.8 fusion.63
  558.0 18.1 %fusion.4 = f32[1280,3840]{1,0:T(8,128)} fusion(bf16[1024,3840]{1,0:T(8,128)(2,1)} %attn_bwd.3, bf16[1024,3840]{1,0:T(8,128)(2,1)} %attn_bwd.2, pred[]{:T(512)S(6)} %eq.21, bf16[1024,1280]{1,0:T(8,128)(2,1)S(1)} %copy-done.12, bf16[1024,1280]{1,0:T(8,128)(2,1)S(1)} %copy-done.3, f32[1280]{0:T(1024)S(1)} %get-tuple-element.36, f32[1024]{0:T(1024)S(1)} %add_rsqrt_fusion.2), kind=kOutput, calls=%fused_computation.9 | convolution fusion | flops 10076815360 | bytes 40641536 | tf_op jit(solution)/shard_map/dot_general | solution.py:22
  576.1 10.8 convolution_add_fusion.1
  587.0 21.2 %convolution_add_fusion = f32[1280,3840]{1,0:T(8,128)} fusion(f32[1280,3840]{1,0:T(8,128)} %fusion.4, bf16[1024,1280]{1,0:T(8,128)(2,1)} %collective-permute-done.6, bf16[1024,3840]{1,0:T(8,128)(2,1)} %collective-permute-done.7), kind=kOutput, calls=%fused_computation | convolution fusion | flops 10071244800 | bytes 49807360 | tf_op jit(solution)/shard_map/dot_general | solution.py:22
  608.2 10.8 broadcast_select_fusion
  620.0 17.4 %fusion.47 = f32[1280]{0:T(1024)S(1)} fusion(bf16[16,64,1280]{2,1,0:T(8,128)(2,1)S(1)} %copy-done.6, bf16[1024,3840]{1,0:T(8,128)(2,1)} %attn_bwd.3, bf16[2,1280,3840]{2,1,0:T(8,128)(2,1)} %all-gather.9.cloned.1.call-done, f32[1024]{0:T(1024)S(1)} %rsqrt.44), kind=kOutput, calls=%fused_computation.65 | convolution fusion | flops 10071571456 | bytes 20325376 | tf_op jit(solution)/shard_map/dot_general | solution.py:22
  647.4 150.0 %all-gather.15.cloned.1.call-done = bf16[8,1024,1280]{2,1,0:T(8,128)(2,1)} async-done(((bf16[2,1024,1280]{2,1,0:T(8,128)(2,1)}), bf16[8,1024,1280]{2,1,0:T(8,128)(2,1)}) %all-gather.15.cloned.1.call-update) | async-done | bytes 20971536 | tf_op jit(solution)/shard_map/all_gather | solution.py:443
  797.4 460.7 %mlp_grad.1 = (f32[1280,5120]{1,0:T(8,128)}, f32[5120,1280]{1,0:T(8,128)}) custom-call(s32[131]{0:T(256)} %chunk_table.1.tbl_ref, bf16[8192,1280]{1,0:T(8,128)(2,1)} %bitcast.98, bf16[8192,1280]{1,0:T(8,128)(2,1)} %bitcast.99, bf16[8192,1280]{1,0:T(8,128)(2,1)} %bitcast.100, bf16[8192,1280]{1,0:T(8,128)(2,1)} %bitcast.101, bf16[8192,1280]{1,0:T(8,128)(2,1)} %bitcast.102, ...), custom_call_target="tpu_custom_call" | custom-call | flops 429496729600 | bytes 288358400 | tf_op jit(solution)/shard_map/mlp_grad/pallas_call | solution.py:269
  1258.2 15.2 %copy.20 = f32[1,1280,3840]{2,1,0:T(8,128)} copy(f32[1,1280,3840]{2,1,0:T(8,128)} %get-tuple-element.59) | data formatting | bytes 39321600
  (184 shorter events, 111.5 us)
Async XLA Ops:
  7.2 67.6 %all-gather.9.cloned.1.call-start = ((), (), s32[]{:S(2)}) async-start(), calls=%async_computation | async-start | bytes 29491200 | tf_op jit(solution)/shard_map/all_gather | solution.py:392
  7.9 117.2 %all-gather.11.cloned.1.call-start = ((), (), s32[]{:S(2)}) async-start(), calls=%async_computation.1 | async-start | bytes 9830400 | tf_op jit(solution)/shard_map/all_gather | solution.py:392
  8.0 126.1 %collective-permute-start.1 = (bf16[1,1280,5120]{2,1,0:T(8,128)(2,1)}, bf16[1,1280,5120]{2,1,0:T(8,128)(2,1)}, u32[]{:S(2)}, u32[]{:S(2)}) collective-permute-start(bf16[1,1280,5120]{2,1,0:T(8,128)(2,1)} %own_up_ref.7), channel_id=1, source_target_pairs={{0,1},{1,0},{2,3},{3,2},{4,5},{5,4},{6,7},{7,6}} | collective-permute-start | bytes 39321608 | tf_op jit(solution)/shard_map/ppermute | solution.py:396
  8.8 125.2 %collective-permute-start.2 = (bf16[1,5120,1280]{2,1,0:T(8,128)(2,1)}, bf16[1,5120,1280]{2,1,0:T(8,128)(2,1)}, u32[]{:S(2)}, u32[]{:S(2)}) collective-permute-start(bf16[1,5120,1280]{2,1,0:T(8,128)(2,1)} %own_down_ref.7), channel_id=1, source_target_pairs={{0,1},{1,0},{2,3},{3,2},{4,5},{5,4},{6,7},{7,6}} | collective-permute-start | bytes 39321608 | tf_op jit(solution)/shard_map/ppermute | solution.py:396
  8.9 599.3 %all-gather.13.cloned.1.call-start = ((), (), s32[]{:S(2)}) async-start(), calls=%async_computation.2 | async-start | bytes 13107200 | tf_op jit(solution)/shard_map/all_gather | solution.py:454
  9.0 56.1 %collective-permute-start = (bf16[1,2,1280]{2,1,0:T(2,128)(2,1)S(1)}, bf16[1,2,1280]{2,1,0:T(2,128)(2,1)S(1)}, u32[]{:S(2)}, u32[]{:S(2)}) collective-permute-start(bf16[1,2,1280]{2,1,0:T(2,128)(2,1)S(1)} %pad_maximum_fusion.3), channel_id=1, source_target_pairs={{0,1},{1,0},{2,3},{3,2},{4,5},{5,4},{6,7},{7,6}} | collective-permute-start | bytes 15368 | tf_op jit(solution)/shard_map/ppermute | solution.py:399
  10.9 50.6 %collective-permute-start.3 = (s32[8,128]{1,0:T(8,128)S(1)}, s32[8,128]{1,0:T(8,128)S(1)}, u32[]{:S(2)}, u32[]{:S(2)}) collective-permute-start(s32[8,128]{1,0:T(8,128)S(1)} %broadcast_in_dim.79), channel_id=1, source_target_pairs={{0,1},{1,0},{2,3},{3,2},{4,5},{5,4},{6,7},{7,6}} | collective-permute-start | bytes 12296 | tf_op jit(solution)/shard_map/ppermute | solution.py:412
  11.8 79.7 %copy-start.26 = (f32[16,64]{1,0:T(8,128)}, f32[16,64]{1,0:T(8,128)S(1)}, u32[]{:S(2)}) copy-start(f32[16,64]{1,0:T(8,128)S(1)} %add_rsqrt_fusion) | copy-start | bytes 12292
  62.2 4.5 collective-permute-start.4
  65.2 66.4 %copy-start.22 = (f32[1280]{0:T(1024)}, f32[1280]{0:T(1024)S(1)}, u32[]{:S(2)}) copy-start(f32[1280]{0:T(1024)S(1)} %get-tuple-element.37) | copy-start | bytes 15364
  66.7 4.2 collective-permute-start.5
  332.9 63.7 %slice-start = ((s8[5242880]{0:T(1024)(128)(4,1)}), s8[1048576]{0:T(1024)(128)(4,1)S(1)}, s32[]{:S(2)}) async-start(s8[5242880]{0:T(1024)(128)(4,1)} %bitcast.79), calls=%async_computation.6 | async-start | bytes 2097152
  406.4 201.8 %all-gather.17.cloned.1.call-start = ((), (), s32[]{:S(2)}) async-start(), calls=%async_computation.4 | async-start | bytes 13107200 | tf_op jit(solution)/shard_map/all_gather | solution.py:418
  412.7 384.7 %all-gather.15.cloned.1.call-start = ((), (), s32[]{:S(2)}) async-start(), calls=%async_computation.3 | async-start | bytes 26214400 | tf_op jit(solution)/shard_map/all_gather | solution.py:443
  419.7 5.1 collective-permute-start.10
  427.7 830.5 %all-reduce.4.cloned.1.call-start = ((), (), s32[]{:S(2)}) async-start(), calls=%async_computation.5 | async-start | bytes 52428800 | tf_op jit(solution)/shard_map/psum | solution.py:472
  543.4 43.5 %collective-permute-start.7 = (bf16[1024,3840]{1,0:T(8,128)(2,1)}, bf16[1024,3840]{1,0:T(8,128)(2,1)}, u32[]{:S(2)}, u32[]{:S(2)}) collective-permute-start(bf16[1024,3840]{1,0:T(8,128)(2,1)} %broadcast_select_fusion.1), channel_id=1, source_target_pairs={{0,1},{1,0},{2,3},{3,2},{4,5},{5,4},{6,7},{7,6}} | collective-permute-start | bytes 23592968 | tf_op jit(solution)/shard_map/ppermute | solution.py:437
  547.7 28.4 %collective-permute-start.9 = (bf16[1024,1280]{1,0:T(8,128)(2,1)}, bf16[1024,1280]{1,0:T(8,128)(2,1)}, u32[]{:S(2)}, u32[]{:S(2)}) collective-permute-start(bf16[1024,1280]{1,0:T(8,128)(2,1)} %get-tuple-element.45), channel_id=1, source_target_pairs={{0,1},{1,0},{2,3},{3,2},{4,5},{5,4},{6,7},{7,6}} | collective-permute-start | bytes 7864328 | tf_op jit(solution)/shard_map/ppermute | solution.py:437
  547.7 28.4 %collective-permute-start.8 = (bf16[1024,1280]{1,0:T(8,128)(2,1)}, bf16[1024,1280]{1,0:T(8,128)(2,1)}, u32[]{:S(2)}, u32[]{:S(2)}) collective-permute-start(bf16[1024,1280]{1,0:T(8,128)(2,1)} %broadcast_select_fusion.3), channel_id=1, source_target_pairs={{0,1},{1,0},{2,3},{3,2},{4,5},{5,4},{6,7},{7,6}} | collective-permute-start | bytes 7864328 | tf_op jit(solution)/shard_map/ppermute | solution.py:437
  548.2 38.7 %collective-permute-start.6 = (bf16[1024,1280]{1,0:T(8,128)(2,1)}, bf16[1024,1280]{1,0:T(8,128)(2,1)}, u32[]{:S(2)}, u32[]{:S(2)}) collective-permute-start(bf16[1024,1280]{1,0:T(8,128)(2,1)} %get-tuple-element.43), channel_id=1, source_target_pairs={{0,1},{1,0},{2,3},{3,2},{4,5},{5,4},{6,7},{7,6}} | collective-permute-start | bytes 7864328 | tf_op jit(solution)/shard_map/ppermute | solution.py:437
  619.1 28.4 %collective-permute-start.11 = (bf16[4096,1280]{1,0:T(8,128)(2,1)}, bf16[4096,1280]{1,0:T(8,128)(2,1)}, u32[]{:S(2)}, u32[]{:S(2)}) collective-permute-start(bf16[4096,1280]{1,0:T(8,128)(2,1)} %broadcast_select_fusion), channel_id=1, source_target_pairs={{0,1},{1,0},{2,3},{3,2},{4,5},{5,4},{6,7},{7,6}} | collective-permute-start | bytes 31457288 | tf_op jit(solution)/shard_map/ppermute | solution.py:474
  637.5 1.2 collective-permute-start.12
  638.7 4.0 collective-permute-start.13
  642.8 4.0 collective-permute-start.14
  (39 other events, 536.9 us)
Sparse Core Ops, SparseCore 0:
  9.5 48.4 all-gather.8
  59.5 15.5 all-gather.10
  406.5 100.4 all-gather.12
  508.6 99.3 all-gather.16
  609.7 187.7 all-gather.14
  801.6 448.9 all-reduce.3
